TPU v7x, 768 devices: a whole 4x8x12 slice. The times are simulated.
768 devices in a mesh: ctx: 16 (over z_hi, y), head: 48 (over x, z_lo, core).
Axes of the slice: x: 4, y: 8, z: 12 (z_hi: 2, z_lo: 6; z = z_hi * 6 + z_lo), core: 2. Of those that a mesh axis runs over, the one named last changes fastest.
Arguments:
- queries: bfloat16 [2048, 18432], P('ctx', 'head'), may hold values from -10 to 10
- latent: bfloat16 [2048, 576], P('ctx'), may hold values from -10 to 10
- block_of: int32 [32], replicated, may hold values from 0 to 31, each once
- key_up: bfloat16 [96, 128, 512], P('head'), may hold values from -0.5 to 0.5
- value_up: bfloat16 [96, 512, 128], P('head'), may hold values from -0.25 to 0.25
- out_grad: bfloat16 [2048, 12288], P('ctx', 'head'), may hold values from -6 to 6
Outputs:
- attended: bfloat16 [2048, 12288], P('ctx', 'head')
- query_grad: bfloat16 [2048, 18432], P('ctx', 'head')
- latent_grad: float32 [2048, 576], P('ctx')
Inputs may be any that keep to these rules, and one draw needn't show every extreme that they name: `block_of`: a permutation of the 32 blocks.
All inputs are finite; a program needn't handle non-finite values.
Results may differ from a plain program's by a relative error of at most 0.0099.
Values may be sent and summed in bfloat16 or wider, within the bound.
A program may use at most 64 MiB of HBM per device.

v0:
```python
import math

import jax
import jax.numpy as jnp
from jax import lax
from jax.sharding import PartitionSpec as P

BLK_DEV = 2


def joined_along(tiles, dim):
    tiles = jnp.moveaxis(tiles, 0, dim)
    dims = tiles.shape
    return tiles.reshape(*dims[:dim], dims[dim] * dims[dim + 1], *dims[dim + 2 :])


def sent_to_all(array, axis):
    copies = jnp.broadcast_to(array, (lax.axis_size(axis), *array.shape))
    return lax.all_to_all(copies, axis, split_axis=0, concat_axis=0, tiled=True)


def collect(array, axis, dim):
    return joined_along(sent_to_all(array, axis), dim)


def on_device(queries, latent, block_of, key_up, value_up, out_grad):
    local_rows = queries.shape[0]
    head_count = key_up.shape[0]
    nope_width = key_up.shape[1]
    latent_width = key_up.shape[2]
    joined_width = latent.shape[1]
    rope_width = joined_width - latent_width
    value_width = value_up.shape[2]
    score_scale = 1.0 / math.sqrt(nope_width + rope_width)
    all_latent = lax.all_gather(latent, "ctx", axis=0, tiled=True)
    total_rows = all_latent.shape[0]
    block_rows = local_rows // BLK_DEV
    row_index = jnp.arange(total_rows, dtype=jnp.int32)
    owner = (row_index // block_rows)[:, None] == jnp.arange(block_of.shape[0], dtype=jnp.int32)[
        None, :
    ]
    all_positions = (
        jnp.sum(jnp.where(owner, block_of[None, :], 0), axis=1) * block_rows
        + row_index % block_rows
    )
    my_positions = lax.dynamic_slice_in_dim(
        all_positions, lax.axis_index("ctx") * local_rows, local_rows
    )
    visible = all_positions[None, :] <= my_positions[:, None]
    query_heads = jnp.transpose(
        queries.reshape(local_rows, head_count, nope_width + rope_width), (1, 0, 2)
    )
    q_latent = jnp.einsum(
        "htn,hnl->htl", query_heads[:, :, :nope_width], key_up, preferred_element_type=jnp.float32
    ).astype(jnp.bfloat16)
    q_joined = jnp.concatenate([q_latent, query_heads[:, :, nope_width:]], axis=2)
    scores = (
        jnp.einsum("htw,kw->htk", q_joined, all_latent, preferred_element_type=jnp.float32)
        * score_scale
    )
    scores = jnp.where(visible[None], scores, -1e30)
    row_max = jnp.max(scores, axis=2, keepdims=True)
    expo = jnp.exp(scores - row_max)
    probs = expo / jnp.sum(expo, axis=2, keepdims=True)
    probs_low = probs.astype(jnp.bfloat16)
    latent_part = all_latent[:, :latent_width]
    out_latent = jnp.einsum(
        "htk,kl->htl", probs_low, latent_part, preferred_element_type=jnp.float32
    ).astype(jnp.bfloat16)
    attended = jnp.einsum(
        "htl,hlv->htv", out_latent, value_up, preferred_element_type=jnp.float32
    ).astype(jnp.bfloat16)
    attended = jnp.transpose(attended, (1, 0, 2)).reshape(local_rows, head_count * value_width)
    grad_heads = jnp.transpose(out_grad.reshape(local_rows, head_count, value_width), (1, 0, 2))
    grad_latent = jnp.einsum(
        "htv,hlv->htl", grad_heads, value_up, preferred_element_type=jnp.float32
    ).astype(jnp.bfloat16)
    grad_probs = jnp.einsum(
        "htl,kl->htk", grad_latent, latent_part, preferred_element_type=jnp.float32
    )
    delta = jnp.sum(probs * grad_probs, axis=2, keepdims=True)
    grad_scores = (probs * (grad_probs - delta) * score_scale).astype(jnp.bfloat16)
    grad_joined = jnp.einsum(
        "htk,kw->htw", grad_scores, all_latent, preferred_element_type=jnp.float32
    )
    grad_nope = jnp.einsum(
        "htl,hnl->htn",
        grad_joined[:, :, :latent_width].astype(jnp.bfloat16),
        key_up,
        preferred_element_type=jnp.float32,
    ).astype(jnp.bfloat16)
    grad_query = jnp.concatenate(
        [grad_nope, grad_joined[:, :, latent_width:].astype(jnp.bfloat16)], axis=2
    )
    query_grad = jnp.transpose(grad_query, (1, 0, 2)).reshape(
        local_rows, head_count * (nope_width + rope_width)
    )
    key_terms = jnp.einsum("htk,htw->kw", grad_scores, q_joined, preferred_element_type=jnp.float32)
    value_terms = jnp.einsum(
        "htk,htl->kl", probs_low, grad_latent, preferred_element_type=jnp.float32
    )
    key_terms = key_terms + jnp.pad(value_terms, ((0, 0), (0, rope_width)))
    flat_terms = key_terms.reshape(total_rows * joined_width)
    piece = lax.psum_scatter(flat_terms, ("ctx", "head"), scatter_dimension=0, tiled=True)
    whole_piece = collect(piece, "head", 0)
    latent_grad = whole_piece.reshape(local_rows, joined_width)
    return (attended, query_grad, latent_grad)


def solution(mesh):
    return jax.shard_map(
        on_device,
        mesh=mesh,
        in_specs=(
            P("ctx", "head"),
            P("ctx", None),
            P(),
            P("head", None, None),
            P("head", None, None),
            P("ctx", "head"),
        ),
        out_specs=(P("ctx", "head"), P("ctx", "head"), P("ctx", None)),
        check_vma=False,
    )
```

profile of v0, /device:TPU:1, one launch (start us, length us, event | category | flops | bytes accessed | tf_op | source)
XLA Modules:
  0.0 706.1 jit_solution(17374629649571115709)
XLA Ops:
  7.2 0.0 all-gather.2.cloned.1.call-start
  7.2 0.7 all-gather.2.cloned.1.call-update
  7.9 0.0 all-reduce.4.cloned.1.call-start
  8.0 1.0 copy.45
  9.0 0.1 copy.46
  9.1 0.8 select_reduce_fusion
  9.9 0.1 dynamic_slice.3
  10.0 1.2 convolution_convert_fusion.1
  11.2 1.1 convolution_convert_fusion
  12.2 0.2 broadcast_compare_fusion
  12.5 135.1 %all-gather.2.cloned.1.call-done = bf16[2048,576]{0,1:T(8,128)(2,1)} async-done(((bf16[128,576]{0,1:T(8,128)(2,1)}), bf16[2048,576]{0,1:T(8,128)(2,1)}) %all-gather.2.cloned.1.call-update) | async-done | bytes 2359312 | tf_op jit(solution)/shard_map/all_gather | solution.py:35
  147.6 2.8 fusion.3
  150.3 0.7 fusion.49
  151.0 0.7 copy-done.1
  151.7 5.3 convolution_bitcast_fusion
  157.0 3.6 fusion.13
  160.6 7.0 bitcast_add_fusion
  167.6 5.8 copy.55
  173.4 7.1 %reshape.86 = f32[1179648]{0:T(1024)} reshape(f32[2048,576]{1,0:T(8,128)} %copy.55) | data formatting | bytes 9437184 | tf_op jit(solution)/shard_map/reshape | solution.py:103
  180.5 489.0 %all-reduce.4.cloned.1.call-done = f32[1179648]{0:T(1024)} async-done(((f32[1179648]{0:T(1024)}), f32[1179648]{0:T(1024)}) %all-reduce.4.cloned.1.call-update) | async-done | bytes 4718608
  669.6 0.8 dynamic-slice
  670.4 0.9 broadcast_in_dim.40
  671.2 9.7 %all-to-all-start = ((f32[48,1,1536]{2,1,0:T(1,128)}), f32[48,1,1536]{2,1,0:T(1,128)S(1)}, u32[]{:S(2)}, u32[]{:S(2)}) async-start(f32[48,1,1536]{2,1,0:T(1,128)} %broadcast_in_dim.40), calls=%async_computation | async-start | bytes 589824 | tf_op jit(solution)/shard_map/all_to_all | solution.py:19
  680.9 4.2 fusion.26
  685.1 0.7 copy.56
  685.9 4.3 fusion.19
  690.2 0.2 convolution_convert_fusion.2
  690.4 0.8 copy.57
  691.2 6.2 all-to-all-done
  697.4 0.7 reduce
  698.1 0.2 reshape_reshape.3
  698.4 0.9 copy.58
  (11 shorter events, 0.1 us)
Async XLA Ops:
  7.2 4.0 copy-start
  7.2 140.4 %all-gather.2.cloned.1.call-start = ((), (), s32[]{:S(2)}) async-start(), calls=%async_computation.1 | async-start | bytes 2506752 | tf_op jit(solution)/shard_map/all_gather | solution.py:35
  7.9 661.7 %all-reduce.4.cloned.1.call-start = ((), (), s32[]{:S(2)}) async-start(), calls=%async_computation.2 | async-start | bytes 9437184
  150.3 1.4 copy-start.1
  671.2 26.2 %all-to-all-start = ((f32[48,1,1536]{2,1,0:T(1,128)}), f32[48,1,1536]{2,1,0:T(1,128)S(1)}, u32[]{:S(2)}, u32[]{:S(2)}) async-start(f32[48,1,1536]{2,1,0:T(1,128)} %broadcast_in_dim.40), calls=%async_computation | async-start | bytes 589824 | tf_op jit(solution)/shard_map/all_to_all | solution.py:19
  685.9 4.3 copy-start.2
Sparse Core Ops, SparseCore 0:
  11.6 135.8 all-gather.1
  180.7 488.8 all-reduce.3
where the time goes:
time: 707 us; the launch traced here: 706 us
  waiting for transfers between devices  631 us (89%)
  matrix products  29.6 us (4%)
  local copies, waits for them, and re-layouts  19.1 us (3%)
  between operations  14.2 us (2%)
  starting transfers between devices  9.78 us (1%)
    unnamed x3, waiting for transfers between devices  490 us
    all_gather x1, waiting for transfers between devices, on_device(): all_latent = lax.all_gather(latent, 'ctx', axis=0, tiled=True)  135 us
  transfers between devices with their start and end apart: 3, of which 3 were waited for; matrix products, arithmetic and copies ran while one was open for 2% of the time, Pallas kernels for 0%

commit v1 on v0

v1 whole, which is shorter than its diff:
```python
import functools
import math

import jax
import jax.numpy as jnp
from jax import lax
from jax.experimental import pallas as pl
from jax.experimental.pallas import tpu as pltpu
from jax.sharding import PartitionSpec as P

MESH = pl.DeviceIdType.MESH
NX, NY, NZH, NZL, NC = 4, 8, 2, 6, 2
NS = NX * NC
NP = NZH * NY
SR = 16
BF = jnp.bfloat16
F32 = jnp.float32


class Place:
    def __init__(self):
        c = lax.axis_index("ctx")
        h = lax.axis_index("head")
        self.c, self.h = c, h
        self.zh, self.y = c // NY, lax.rem(c, NY)
        self.k = lax.rem(h, NC)
        self.zl = lax.rem(h // NC, NZL)
        self.x = h // (NC * NZL)

    def at(self, zh=None, y=None, x=None, zl=None, k=None):
        zh = self.zh if zh is None else zh
        y = self.y if y is None else y
        x = self.x if x is None else x
        zl = self.zl if zl is None else zl
        k = self.k if k is None else k
        return (zh * NY + y, (x * NZL + zl) * NC + k)

    def partner(self):
        return self.at(k=1 - self.k)

    def mirror(self):
        return self.at(zh=1 - self.zh, zl=NZL - 1 - self.zl)

    def y_peer(self, d):
        return self.at(y=lax.rem(self.y + d, NY))

    def x_peer(self, d, other=False):
        return self.at(x=lax.rem(self.x + d, NX), k=1 - self.k if other else self.k)

    def zl_peer(self, d):
        return self.at(zl=lax.rem(self.zl + d, NZL))


def greet(peers):
    barrier = pltpu.get_barrier_semaphore()
    for peer in peers:
        pl.semaphore_signal(barrier, inc=1, device_id=peer, device_id_type=MESH)
    pl.semaphore_wait(barrier, len(peers))


def remote(src, dst, send_sem, recv_sem, peer):
    return pltpu.make_async_remote_copy(
        src_ref=src, dst_ref=dst, send_sem=send_sem, recv_sem=recv_sem,
        device_id=peer, device_id_type=MESH,
    )


Y_ORDER = (4, 3, 5, 2, 6, 1, 7)
X_ORDER = (2, 1, 3)


def gather_kernel(lat, out, ysend, yrecv, msend, mrecv, xsend, xrecv, dsend, drecv):
    me = Place()
    greet(
        [me.partner(), me.mirror()]
        + [me.y_peer(d) for d in range(1, NY)]
        + [me.x_peer(d) for d in range(1, NX)]
    )
    s = me.k * NX + me.x
    mine = lat.at[s]
    to_mirror = remote(mine, out.at[s, me.c], msend, mrecv, me.mirror())
    to_mirror.start()
    first = []
    for d in Y_ORDER:
        copy = remote(mine, out.at[s, me.c], ysend.at[0, d - 1], yrecv.at[0, d - 1], me.y_peer(d))
        copy.start()
        first.append(copy)
    out[s, me.c] = lat[s]
    far = 1 - me.zh

    to_mirror.wait()
    second = []
    got = out.at[s, far * NY + me.y]
    for d in Y_ORDER:
        copy = remote(got, got, ysend.at[1, d - 1], yrecv.at[1, d - 1], me.y_peer(d))
        copy.start()
        second.append(copy)

    def spread(group, half):
        part = out.at[s, pl.ds(half * NY, NY)]
        copies = []
        for d in X_ORDER:
            copy = remote(part, part, xsend.at[group, d - 1], xrecv.at[group, d - 1], me.x_peer(d))
            copy.start()
            copies.append(copy)
        cross = remote(part, part, dsend.at[group, 0], drecv.at[group, 0], me.partner())
        cross.start()
        return copies, [cross]

    def relay(group, half, copies, crosses):
        for d, copy in zip(X_ORDER, copies):
            copy.wait()
            source = me.k * NX + lax.rem(me.x + NX - d, NX)
            part = out.at[source, pl.ds(half * NY, NY)]
            cross = remote(part, part, dsend.at[group, d], drecv.at[group, d], me.partner())
            cross.start()
            crosses.append(cross)

    for copy in first:
        copy.wait()
    near_x, near_d = spread(0, me.zh)
    for copy in second:
        copy.wait()
    far_x, far_d = spread(1, far)
    relay(0, me.zh, near_x, near_d)
    relay(1, far, far_x, far_d)
    for cross in near_d + far_d:
        cross.wait()


def gather(latent):
    width = latent.shape[1]
    return pl.pallas_call(
        gather_kernel,
        out_shape=jax.ShapeDtypeStruct((NS, NP, SR, width), BF),
        in_specs=[pl.BlockSpec(memory_space=pltpu.VMEM)],
        out_specs=pl.BlockSpec(memory_space=pltpu.VMEM),
        scratch_shapes=[
            pltpu.SemaphoreType.DMA((2, NY - 1)),
            pltpu.SemaphoreType.DMA((2, NY - 1)),
            pltpu.SemaphoreType.DMA,
            pltpu.SemaphoreType.DMA,
            pltpu.SemaphoreType.DMA((2, NX - 1)),
            pltpu.SemaphoreType.DMA((2, NX - 1)),
            pltpu.SemaphoreType.DMA((2, NX)),
            pltpu.SemaphoreType.DMA((2, NX)),
        ],
        compiler_params=pltpu.CompilerParams(collective_id=0, has_side_effects=True),
    )(latent.reshape(NS, SR, width))


NT = (((1,), (1,)), ((), ()))
TN = (((0,), (0,)), ((), ()))
KC = 512


def attention_kernel(
    scale, q_ref, g_ref, ku_ref, vu_ref, lat_ref, kpos_ref, qpos_ref, att_ref, qg_ref, kt_ref,
    qr_ref, ql_ref, gl_ref, s_ref, gp_ref,
):
    heads, nope, width = ku_ref.shape
    value = vu_ref.shape[2]
    rows = q_ref.shape[0]
    keys = lat_ref.shape[0]
    rope = lat_ref.shape[1] - width
    head_width = nope + rope
    chunks = [pl.ds(i * KC, KC) for i in range(keys // KC)]
    for h in range(heads):
        at = pl.ds(h * rows, rows)
        qn = q_ref[:, h * head_width : h * head_width + nope]
        ql_ref[at, :] = jnp.dot(qn, ku_ref[h], preferred_element_type=F32).astype(BF)
        qr_ref[at, :] = q_ref[:, h * head_width + nope : (h + 1) * head_width]
        gl_ref[at, :] = lax.dot_general(
            g_ref[:, h * value : (h + 1) * value], vu_ref[h], NT, preferred_element_type=F32
        ).astype(BF)
    low = jnp.full((heads * rows, 1), -1e30, F32)
    for at in chunks:
        part = lax.dot_general(
            ql_ref[...], lat_ref[at, :width], NT, preferred_element_type=F32
        ) + lax.dot_general(qr_ref[...], lat_ref[at, width:], NT, preferred_element_type=F32)
        seen = kpos_ref[:, at] <= qpos_ref[...]
        part = part * scale
        for h in range(heads):
            s_ref[pl.ds(h * rows, rows), at] = jnp.where(
                seen, part[h * rows : (h + 1) * rows], -1e30
            )
        low = jnp.maximum(low, jnp.max(s_ref[:, at], axis=1, keepdims=True))
        gp_ref[:, at] = lax.dot_general(
            gl_ref[...], lat_ref[at, :width], NT, preferred_element_type=F32
        )
    total = jnp.zeros((heads * rows, 1), F32)
    delta = jnp.zeros((heads * rows, 1), F32)
    for at in chunks:
        expo = jnp.exp(s_ref[:, at] - low)
        s_ref[:, at] = expo
        total += jnp.sum(expo, axis=1, keepdims=True)
        delta += jnp.sum(expo * gp_ref[:, at], axis=1, keepdims=True)
    inverse = 1.0 / total
    delta = delta * inverse
    out = jnp.zeros((heads * rows, width), F32)
    joined = jnp.zeros((heads * rows, width), F32)
    joined_rope = jnp.zeros((heads * rows, rope), F32)
    for at in chunks:
        probs = s_ref[:, at] * inverse
        probs_low = probs.astype(BF)
        grads = (probs * (gp_ref[:, at] - delta) * scale).astype(BF)
        out += jnp.dot(probs_low, lat_ref[at, :width], preferred_element_type=F32)
        joined += jnp.dot(grads, lat_ref[at, :width], preferred_element_type=F32)
        joined_rope += jnp.dot(grads, lat_ref[at, width:], preferred_element_type=F32)
        kt_ref[at, :width] = (
            lax.dot_general(grads, ql_ref[...], TN, preferred_element_type=F32)
            + lax.dot_general(probs_low, gl_ref[...], TN, preferred_element_type=F32)
        ).astype(BF)
        kt_ref[at, width:] = lax.dot_general(
            grads, qr_ref[...], TN, preferred_element_type=F32
        ).astype(BF)
    for h in range(heads):
        part = slice(h * rows, (h + 1) * rows)
        att_ref[:, h * value : (h + 1) * value] = jnp.dot(
            out[part].astype(BF), vu_ref[h], preferred_element_type=F32
        ).astype(BF)
        qg_ref[:, h * head_width : h * head_width + nope] = lax.dot_general(
            joined[part].astype(BF), ku_ref[h], NT, preferred_element_type=F32
        ).astype(BF)
        qg_ref[:, h * head_width + nope : (h + 1) * head_width] = joined_rope[part].astype(BF)


def attention(scale, queries, out_grad, key_up, value_up, all_latent, key_pos, my_pos):
    rows = queries.shape[0]
    heads, nope, width = key_up.shape
    keys, joined = all_latent.shape
    both = heads * rows
    vmem = pl.BlockSpec(memory_space=pltpu.VMEM)
    return pl.pallas_call(
        functools.partial(attention_kernel, scale),
        out_shape=(
            jax.ShapeDtypeStruct(out_grad.shape, BF),
            jax.ShapeDtypeStruct(queries.shape, BF),
            jax.ShapeDtypeStruct((keys, joined), BF),
        ),
        in_specs=[vmem] * 7,
        out_specs=(vmem,) * 3,
        scratch_shapes=[
            pltpu.VMEM((both, joined - width), BF),
            pltpu.VMEM((both, width), BF),
            pltpu.VMEM((both, width), BF),
            pltpu.VMEM((both, keys), F32),
            pltpu.VMEM((both, keys), F32),
        ],
        compiler_params=pltpu.CompilerParams(vmem_limit_bytes=40 * 1024 * 1024),
        cost_estimate=pl.CostEstimate(
            flops=2 * both * keys * (6 * width), bytes_accessed=8 << 20, transcendentals=both * keys
        ),
    )(queries, out_grad, key_up, value_up, all_latent, key_pos, my_pos)


def reduce_kernel(
    terms, out, pair_in, x_out, x_in, y_out, y_in, m_out, m_in, z_in,
    dsend, drecv, xsend, xrecv, ysend, yrecv, msend, mrecv, zsend, zrecv, osend, orecv,
):
    me = Place()
    greet(
        [me.partner(), me.mirror()]
        + [me.y_peer(d) for d in range(1, NY)]
        + [me.x_peer(d) for d in range(1, NX)]
        + [me.x_peer(d, True) for d in range(1, NX)]
        + [me.zl_peer(d) for d in range(1, NZL)]
    )
    pairs = {}
    for d in X_ORDER + (0,):
        x = lax.rem(me.x + d, NX)
        copy = remote(terms.at[1 - me.k, x], pair_in.at[d], dsend.at[d], drecv.at[d], me.partner())
        copy.start()
        pairs[d] = copy
    moves = []
    for d in X_ORDER:
        x = lax.rem(me.x + d, NX)
        pairs[d].wait()
        x_out[d - 1] = (terms[me.k, x].astype(F32) + pair_in[d].astype(F32)).astype(BF)
        copy = remote(x_out.at[d - 1], x_in.at[d - 1], xsend.at[d - 1], xrecv.at[d - 1], me.x_peer(d))
        copy.start()
        moves.append(copy)
    pairs[0].wait()
    for copy in moves:
        copy.wait()
    for d in range(NY):
        y = lax.rem(me.y + d, NY)
        part = terms[me.k, me.x, :, y].astype(F32) + pair_in[0, :, y].astype(F32)
        for i in range(NX - 1):
            part += x_in[i, :, y].astype(F32)
        y_out[d] = part.astype(BF)
    moves = []
    for d in Y_ORDER:
        copy = remote(y_out.at[d], y_in.at[d - 1], ysend.at[d - 1], yrecv.at[d - 1], me.y_peer(d))
        copy.start()
        moves.append(copy)
    for copy in moves:
        copy.wait()

    def of_half(zh):
        part = y_out[0, zh].astype(F32)
        for i in range(NY - 1):
            part += y_in[i, zh].astype(F32)
        return part

    m_out[...] = of_half(1 - me.zh).astype(BF)
    to_mirror = remote(m_out, m_in, msend, mrecv, me.mirror())
    to_mirror.start()
    own = of_half(me.zh)
    to_mirror.wait()
    z_in[me.zl] = (own + m_in[...].astype(F32)).astype(BF)
    moves = []
    for d in (3, 2, 4, 1, 5):
        copy = remote(
            z_in.at[me.zl], z_in.at[me.zl], zsend.at[d - 1], zrecv.at[d - 1], me.zl_peer(d)
        )
        copy.start()
        moves.append(copy)
    for copy in moves:
        copy.wait()
    part = z_in[0].astype(F32)
    for i in range(1, NZL):
        part += z_in[i].astype(F32)
    s = me.k * NX + me.x
    out[s] = part.astype(BF)
    moves = []
    for j, peer in enumerate(
        [me.x_peer(d) for d in X_ORDER] + [me.x_peer(d, True) for d in X_ORDER] + [me.partner()]
    ):
        copy = remote(out.at[s], out.at[s], osend.at[j], orecv.at[j], peer)
        copy.start()
        moves.append(copy)
    for copy in moves:
        copy.wait()


def reduction(terms):
    width = terms.shape[-1]
    vmem = pl.BlockSpec(memory_space=pltpu.VMEM)
    dma = pltpu.SemaphoreType.DMA
    region = (NZH, NY, SR, width)
    return pl.pallas_call(
        reduce_kernel,
        out_shape=jax.ShapeDtypeStruct((NS, SR, width), BF),
        in_specs=[vmem],
        out_specs=vmem,
        scratch_shapes=[
            pltpu.VMEM((NX, *region), BF),
            pltpu.VMEM((NX - 1, *region), BF),
            pltpu.VMEM((NX - 1, *region), BF),
            pltpu.VMEM((NY, NZH, SR, width), BF),
            pltpu.VMEM((NY - 1, NZH, SR, width), BF),
            pltpu.VMEM((SR, width), BF),
            pltpu.VMEM((SR, width), BF),
            pltpu.VMEM((NZL, SR, width), BF),
            dma((NX,)), dma((NX,)),
            dma((NX - 1,)), dma((NX - 1,)),
            dma((NY - 1,)), dma((NY - 1,)),
            dma, dma,
            dma((NZL - 1,)), dma((NZL - 1,)),
            dma((7,)), dma((7,)),
        ],
        compiler_params=pltpu.CompilerParams(collective_id=1, has_side_effects=True),
    )(terms.reshape(NC, NX, *region))


def on_device(queries, latent, block_of, key_up, value_up, out_grad):
    rows, joined = latent.shape
    nope, width = key_up.shape[1:]
    scale = 1.0 / math.sqrt(nope + joined - width)
    block = rows // 2
    per_block = block // SR
    all_latent = gather(latent).reshape(NP * rows, joined)
    starts = jnp.transpose(block_of.reshape(NP, 2)) * block
    key_pos = (
        starts[:, None, :, None]
        + (jnp.arange(per_block, dtype=jnp.int32) * SR)[None, :, None, None]
        + jnp.arange(SR, dtype=jnp.int32)[None, None, None, :]
    ).reshape(1, NP * rows)
    mine = lax.dynamic_slice_in_dim(block_of, lax.axis_index("ctx") * 2, 2) * block
    my_pos = (mine[:, None] + jnp.arange(block, dtype=jnp.int32)[None, :]).reshape(rows, 1)
    attended, query_grad, terms = attention(
        scale, queries, out_grad, key_up, value_up, all_latent, key_pos, my_pos
    )
    latent_grad = reduction(terms).reshape(rows, joined).astype(F32)
    return attended, query_grad, latent_grad


def solution(mesh):
    return jax.shard_map(
        on_device,
        mesh=mesh,
        in_specs=(
            P("ctx", "head"),
            P("ctx", None),
            P(),
            P("head", None, None),
            P("head", None, None),
            P("ctx", "head"),
        ),
        out_specs=(P("ctx", "head"), P("ctx", "head"), P("ctx", None)),
        check_vma=False,
    )
```

time: 707 us -> 109 us (0.15)
  waiting for transfers between devices: 631 us -> 0 us
  Pallas kernels: 0 us -> 99 us
  matrix products: 29.6 us -> 0 us
  between operations: 14.2 us -> 0.75 us
  local copies, waits for them, and re-layouts: 19.1 us -> 6.24 us
  starting transfers between devices: 9.78 us -> 0 us
    unnamed x3 -> x0, waiting for transfers between devices: 490 us -> none
    all_gather x1 -> x0, waiting for transfers between devices: 135 us -> none  [on_device(): all_latent = lax.all_gather(latent, 'ctx', axis=0, tiled=True)]
    pallas_call x0 -> x3, Pallas kernels: none -> 99 us  [the longest x1 49.4 us: reduction(): pl.pallas_call(reduce_kernel, out_shape=jax.ShapeDtypeStruct((NS, SR, wid...]
    dot_general x9 -> x0, matrix products: 29.6 us -> none  [the longest x1 6.97 us: on_device(): jnp.einsum('htk,htw->kw', grad_scores, q_joined, preferred_element_type=j...]
    all_to_all x1 -> x0, starting transfers between devices: 9.7 us -> none  [sent_to_all(): return lax.all_to_all(copies, axis, split_axis=0, concat_axis=0, tiled=True)]
    reshape x2 -> x0, local copies, waits for them, and re-layouts: 7.23 us -> none  [the longest x1 7.12 us: on_device(): flat_terms = key_terms.reshape(total_rows * joined_width)]
  transfers between devices with their start and end apart: 3 -> 0, of which waited for: 3 -> 0; matrix products, arithmetic and copies ran while one was open for 2% -> 0% of each run, Pallas kernels for 0% -> 0%
where the time goes in v1:
time: 109 us
  Pallas kernels  99 us (91%)
  local copies, waits for them, and re-layouts  6.24 us (6%)
  other arithmetic  2.63 us (2%)
    pallas_call x1, Pallas kernels, reduction(): pl.pallas_call(reduce_kernel, out_shape=jax.ShapeDtypeStruct((NS, SR, wid...  49.4 us
    pallas_call x1, Pallas kernels, gather(): pl.pallas_call(gather_kernel, out_shape=jax.ShapeDtypeStruct((NS, NP, SR,...  43.6 us
    pallas_call x1, Pallas kernels, attention(): pl.pallas_call(functools.partial(attention_kernel, scale), out_shape=(jax...  6.03 us
    unnamed x14, local copies, waits for them, and re-layouts  5.85 us

profile of v1, /device:TPU:1, one launch (start us, length us, event | category | flops | bytes accessed | tf_op | source)
XLA Modules:
  0.0 108.7 jit_solution(6251739957588888901)
XLA Ops:
  0.6 0.0 copy-start.5
  0.6 0.0 copy-start.3
  0.7 0.0 copy-start.2
  0.7 0.0 copy-start.4
  0.7 0.8 dynamic-slice_multiply_fusion
  1.5 0.1 iota_add_fusion.1
  1.5 0.7 broadcast_multiply_fusion
  2.2 0.1 mul.27
  2.3 0.1 copy.14
  2.4 0.1 broadcast_add_fusion
  2.4 0.1 iota_add_fusion
  2.5 0.1 add.73.kpos_ref
  2.6 0.1 add.79.qpos_ref
  2.8 1.7 %copy.13 = bf16[128,576]{1,0:T(8,128)(2,1)} copy(bf16[128,576]{0,1:T(8,128)(2,1)} %param.7) | data formatting | bytes 294912 | tf_op args[1]
  4.5 43.6 %shard_map.85 = bf16[8,16,16,576]{3,2,1,0:T(8,128)(2,1)} custom-call(bf16[8,16,576]{2,1,0:T(8,128)(2,1)} %bitcast.11), custom_call_target="tpu_custom_call" | custom-call | tf_op jit(solution)/shard_map/pallas_call | solution.py:133
  48.1 0.0 copy-done.5
  48.1 0.0 copy-done.3
  48.1 0.0 copy-done.2
  48.1 0.0 copy-done.4
  48.2 0.0 copy-start
  48.2 1.7 %copy-done = bf16[8,16,16,576]{3,2,1,0:T(8,128)(2,1)S(1)} copy-done((bf16[8,16,16,576]{3,2,1,0:T(8,128)(2,1)S(1)}, bf16[8,16,16,576]{3,2,1,0:T(8,128)(2,1)}, u32[]{:S(2)}) %copy-start) | copy-done | bytes 2359320
  49.9 6.0 %shard_map.86 = (bf16[128,256]{1,0:T(8,128)(2,1)}, bf16[128,384]{1,0:T(8,128)(2,1)}, bf16[2048,576]{1,0:T(8,128)(2,1)S(1)}) custom-call(bf16[128,384]{1,0:T(8,128)(2,1)S(1)} %copy-done.4, bf16[128,256]{1,0:T(8,128)(2,1)S(1)} %copy-done.5, bf16[2,128,512]{2,1,0:T(8,128)(2,1)S(1)} %copy-done.2, bf16[2,512,128]{2,1,0:T(8,128)(2,1)S(1)} %copy-done.3, ...), custom_call_target="tpu_custom_call" | custom-call | flops 3221225472 | bytes 8388608 | tf_op jit(solution)/shard_map/pallas_call | solution.py:234
  55.9 0.0 copy-start.1
  55.9 1.5 %copy-done.1 = bf16[2048,576]{1,0:T(8,128)(2,1)} copy-done((bf16[2048,576]{1,0:T(8,128)(2,1)}, bf16[2048,576]{1,0:T(8,128)(2,1)S(1)}, u32[]{:S(2)}) %copy-start.1) | copy-done | bytes 2359320
  57.5 49.4 %shard_map.87 = bf16[8,16,576]{2,1,0:T(8,128)(2,1)} custom-call(bf16[2,4,2,8,16,576]{5,4,3,2,1,0:T(8,128)(2,1)} %bitcast.10), custom_call_target="tpu_custom_call" | custom-call | tf_op jit(solution)/shard_map/pallas_call | solution.py:342
  106.8 0.9 bitcast_convert_fusion
  107.8 0.9 copy.16
  (1 shorter events, 0.0 us)
Async XLA Ops:
  0.6 47.5 %copy-start.5 = (bf16[128,256]{1,0:T(8,128)(2,1)S(1)}, bf16[128,256]{1,0:T(8,128)(2,1)}, u32[]{:S(2)}) copy-start(bf16[128,256]{1,0:T(8,128)(2,1)} %g_ref.1) | copy-start | bytes 196612
  0.6 47.5 %copy-start.3 = (bf16[2,512,128]{2,1,0:T(8,128)(2,1)S(1)}, bf16[2,512,128]{2,1,0:T(8,128)(2,1)}, u32[]{:S(2)}) copy-start(bf16[2,512,128]{2,1,0:T(8,128)(2,1)} %vu_ref.1) | copy-start | bytes 786436
  0.7 47.5 %copy-start.2 = (bf16[2,128,512]{2,1,0:T(8,128)(2,1)S(1)}, bf16[2,128,512]{2,1,0:T(8,128)(2,1)}, u32[]{:S(2)}) copy-start(bf16[2,128,512]{2,1,0:T(8,128)(2,1)} %ku_ref.1) | copy-start | bytes 786436
  0.7 47.5 %copy-start.4 = (bf16[128,384]{1,0:T(8,128)(2,1)S(1)}, bf16[128,384]{1,0:T(8,128)(2,1)}, u32[]{:S(2)}) copy-start(bf16[128,384]{1,0:T(8,128)(2,1)} %q_ref.1) | copy-start | bytes 294916
  48.2 1.7 %copy-start = (bf16[8,16,16,576]{3,2,1,0:T(8,128)(2,1)S(1)}, bf16[8,16,16,576]{3,2,1,0:T(8,128)(2,1)}, u32[]{:S(2)}) copy-start(bf16[8,16,16,576]{3,2,1,0:T(8,128)(2,1)} %shard_map.85) | copy-start | bytes 7077892
  55.9 1.5 %copy-start.1 = (bf16[2048,576]{1,0:T(8,128)(2,1)}, bf16[2048,576]{1,0:T(8,128)(2,1)S(1)}, u32[]{:S(2)}) copy-start(bf16[2048,576]{1,0:T(8,128)(2,1)S(1)} %get-tuple-element.8) | copy-start | bytes 7077892

commit v2 on v0

v2 whole, which is shorter than its diff:
```python
import functools
import math

import jax
import jax.numpy as jnp
from jax import lax
from jax.experimental import pallas as pl
from jax.experimental.pallas import tpu as pltpu
from jax.sharding import PartitionSpec as P

MESH = pl.DeviceIdType.MESH
NX, NY, NZH, NZL, NC = 4, 8, 2, 6, 2
SR = 16
LANES = 128
SLOTS = (0, 1, 7, 2, 6, 3, 5, 4)
SLOT_OF = {j: i for i, j in enumerate(SLOTS)}
HALF = NY // 2
GROUPS = (pl.ds(0, HALF), pl.ds(HALF, HALF))
TILE_OF = ((0, 1, 5, 6), (2, 3, 7, 8))
ROTARY_TILE = 4
TILES = 9
WIDE, NARROW = 5, 4
BF = jnp.bfloat16
F32 = jnp.float32
NT = (((1,), (1,)), ((), ()))
TN = (((0,), (0,)), ((), ()))


class Place:
    def __init__(self):
        self.c = lax.axis_index("ctx")
        h = lax.axis_index("head")
        self.zh, self.y = self.c // NY, lax.rem(self.c, NY)
        self.k = lax.rem(h, NC)
        self.zl = lax.rem(h // NC, NZL)
        self.x = h // (NC * NZL)
        self.odd = lax.rem(self.zl, 2)

    def at(self, dy=0, dx=0, dk=0, pair=0, dzl=0, far=0, mirror=False):
        zh = 1 - self.zh if far else self.zh
        y = lax.rem(self.y + dy, NY)
        x = lax.rem(self.x + dx, NX)
        k = 1 - self.k if dk else self.k
        zl = self.zl
        if mirror:
            zl = NZL - 1 - zl
        if pair:
            zl = zl + 1 - 2 * self.odd
        if dzl:
            zl = lax.rem(zl + dzl, NZL)
        return (zh * NY + y, (x * NZL + zl) * NC + k)


def kernel(
    scale, nope, rope, width, value, heads,
    blocks, lat, q_ref, g_ref, ku_ref, vu_ref,
    att_ref, qg_ref, grad_ref,
    keys, qr_ref, ql_ref, gl_ref, s_ref, gp_ref, p_ref, gs_ref,
    terms, pair_in, x_out, relay_in, direct_in, relay_out, sum_in,
    y_far, y_near, y_far_in, y_near_in, w_ref, z_own, z_out, z_far, final,
    y_send, y_recv, m_send, m_recv, x_send, x_recv, d_send, d_recv,
    p_send, p_recv, rx_send, rx_recv, ry_send, ry_recv, rz_send, rz_recv, f_send, f_recv,
):
    me = Place()
    rows = q_ref.shape[0]
    both = heads * rows
    head_width = nope + rope
    chunk = NC * NY * SR
    pending = []

    def send(src, dst, send_sem, recv_sem, peer):
        copy = pltpu.make_async_remote_copy(
            src_ref=src, dst_ref=dst, send_sem=send_sem, recv_sem=recv_sem,
            device_id=peer, device_id_type=MESH,
        )
        copy.start()
        pending.append(copy)
        return copy

    finals = [
        dict(pair=pair, dk=dk, dx=dx)
        for pair in range(2) for dk in range(NC) for dx in range(NX) if pair or dk or dx
    ]
    peers = (
        [dict(dy=d) for d in range(1, NY)]
        + [dict(dy=d, pair=1) for d in range(1, NY)]
        + finals
        + [dict(dzl=2), dict(dzl=4), dict(far=1), dict(far=1, dzl=2), dict(far=1, dzl=4)]
        + [dict(far=1, mirror=True)]
    )
    barrier = pltpu.get_barrier_semaphore()
    for peer in peers:
        pl.semaphore_signal(barrier, inc=1, device_id=me.at(**peer), device_id_type=MESH)

    for h in range(heads):
        at = pl.ds(h * rows, rows)
        qn = q_ref[:, h * head_width : h * head_width + nope]
        ql_ref[at, :] = jnp.dot(qn, ku_ref[h], preferred_element_type=F32).astype(BF)
        qr_ref[at, :] = q_ref[:, h * head_width + nope : (h + 1) * head_width]
        gl_ref[at, :] = lax.dot_general(
            g_ref[:, h * value : (h + 1) * value], vu_ref[h], NT, preferred_element_type=F32
        ).astype(BF)
    block = rows // 2
    row = lax.broadcasted_iota(jnp.int32, (rows, 1), 0)
    my_pos = jnp.where(row < block, blocks[2 * me.c], blocks[2 * me.c + 1]) * block + lax.rem(
        row, block
    )
    lane = lax.broadcasted_iota(jnp.int32, (1, chunk), 1)
    starts = []
    for zr in range(NZH):
        start = jnp.zeros((1, chunk), jnp.int32)
        for kr in range(NC):
            for slot, j in enumerate(SLOTS):
                zh = 1 - me.zh if zr else me.zh
                k = 1 - me.k if kr else me.k
                owner = zh * NY + lax.rem(me.y + j, NY)
                start = jnp.where(
                    lane // SR == kr * NY + slot, blocks[2 * owner + k] * block, start
                )
        starts.append(start + lax.rem(lane, SR))
    mine = pl.ds(pl.multiple_of((me.k * NX + me.x) * SR, SR), SR)
    keys[0, 0, 0, 0] = lat[mine, :]

    pl.semaphore_wait(barrier, len(peers))

    own = lat.at[mine, :]
    to_mirror = send(own, keys.at[1, 0, 0, 0], m_send, m_recv, me.at(far=1, mirror=True))

    def along_y(zr, src):
        return {
            NY - d: send(
                src, keys.at[zr, 0, 0, SLOT_OF[NY - d]],
                y_send.at[zr, d - 1], y_recv.at[zr, d - 1], me.at(dy=d),
            )
            for d in (7, 1, 6, 2, 5, 3, 4)
        }

    def x_copy(zr, i, src_x, dst_x, group, dx):
        return send(
            keys.at[zr, src_x, 0, GROUPS[group]], keys.at[zr, dst_x, 0, GROUPS[group]],
            x_send.at[zr, i], x_recv.at[zr, i], me.at(dx=dx),
        )

    def cross(zr, xr):
        return send(
            keys.at[zr, xr, 0], keys.at[zr, xr, 1], d_send.at[zr, xr], d_recv.at[zr, xr],
            me.at(dk=1),
        )

    def spread(zr, arrivals):
        for j in SLOTS[1:HALF]:
            arrivals[j].wait_recv()
        a_right = x_copy(zr, 0, 0, 3, 0, 1)
        a_left = x_copy(zr, 1, 0, 1, 0, 3)
        for j in SLOTS[HALF:]:
            arrivals[j].wait_recv()
        b_left = x_copy(zr, 2, 0, 1, 1, 3)
        b_right = x_copy(zr, 3, 0, 3, 1, 1)
        return a_right, a_left, b_left, b_right, cross(zr, 0)

    def forward(zr, moves):
        a_right, a_left, b_left, b_right, _ = moves
        a_right.wait_recv()
        relay_a = x_copy(zr, 4, 3, 2, 0, 1)
        b_left.wait_recv()
        relay_b = x_copy(zr, 5, 1, 2, 1, 3)
        b_right.wait_recv()
        from_left = cross(zr, 3)
        a_left.wait_recv()
        from_right = cross(zr, 1)
        return relay_a, relay_b, from_left, from_right

    def close(zr, relays):
        relays[0].wait_recv()
        relays[1].wait_recv()
        return cross(zr, 2)

    maxima = []

    def score(zr, xr, arrived):
        arrived.wait_recv()
        at = pl.ds((zr * NX + xr) * chunk, chunk)
        k_val = keys[zr, xr].reshape(chunk, width + rope)
        part = lax.dot_general(
            ql_ref[...], k_val[:, :width], NT, preferred_element_type=F32
        ) + lax.dot_general(qr_ref[...], k_val[:, width:], NT, preferred_element_type=F32)
        key_pos = starts[zr] + lax.rem(me.x + xr, NX) * SR
        seen = key_pos <= my_pos
        part = part * scale
        part = jnp.concatenate(
            [jnp.where(seen, part[h * rows : (h + 1) * rows], -1e30) for h in range(heads)], axis=0
        )
        s_ref[:, at] = part
        maxima.append(jnp.max(part, axis=1, keepdims=True))
        gp_ref[:, at] = lax.dot_general(
            gl_ref[...], k_val[:, :width], NT, preferred_element_type=F32
        )

    near = along_y(0, own)
    near_moves = spread(0, near)
    to_mirror.wait_recv()
    far = along_y(1, keys.at[1, 0, 0, 0])
    near_relays = forward(0, near_moves)
    score(0, 0, near_moves[4])
    far_moves = spread(1, far)
    near_last = close(0, near_relays)
    score(0, 3, near_relays[2])
    score(0, 1, near_relays[3])
    far_relays = forward(1, far_moves)
    score(0, 2, near_last)
    score(1, 0, far_moves[4])
    far_last = close(1, far_relays)
    score(1, 3, far_relays[2])
    score(1, 1, far_relays[3])
    score(1, 2, far_last)

    low = functools.reduce(jnp.maximum, maxima)
    total = jnp.zeros((both, 1), F32)
    delta = jnp.zeros((both, 1), F32)
    for i in range(NZH * NX):
        at = pl.ds(i * chunk, chunk)
        expo = jnp.exp(s_ref[:, at] - low)
        s_ref[:, at] = expo
        total += jnp.sum(expo, axis=1, keepdims=True)
        delta += jnp.sum(expo * gp_ref[:, at], axis=1, keepdims=True)
    inverse = 1.0 / total
    delta = delta * inverse

    crossings = {}
    for xr in (2, 1, 3, 0):
        rotary = []
        for zr in range(NZH):
            at = pl.ds((zr * NX + xr) * chunk, chunk)
            probs = s_ref[:, at] * inverse
            probs_low = probs.astype(BF)
            grads = (probs * (gp_ref[:, at] - delta) * scale).astype(BF)
            p_ref[:, at] = probs_low
            gs_ref[:, at] = grads
            wide = lax.dot_general(
                grads, ql_ref[...], TN, preferred_element_type=F32
            ) + lax.dot_general(probs_low, gl_ref[...], TN, preferred_element_type=F32)
            rotary.append(lax.dot_general(grads, qr_ref[...], TN, preferred_element_type=F32))
            for kr in range(NC):
                part = wide[kr * NY * SR : (kr + 1) * NY * SR].astype(BF)
                for t in range(width // LANES):
                    terms[kr, xr, TILE_OF[zr][t]] = part[:, t * LANES : (t + 1) * LANES].reshape(
                        NY, SR, LANES
                    )
        for kr in range(NC):
            cut = slice(kr * NY * SR, (kr + 1) * NY * SR)
            terms[kr, xr, ROTARY_TILE] = (
                jnp.concatenate([r[cut] for r in rotary], axis=1).astype(BF).reshape(NY, SR, LANES)
            )
        crossings[xr] = send(
            terms.at[1, xr], pair_in.at[xr], p_send.at[xr], p_recv.at[xr], me.at(dk=1)
        )

    windows = (
        (pl.ds(4 * (1 - me.odd), WIDE), pl.ds(0, WIDE), WIDE),
        (pl.ds(5 * me.odd, NARROW), pl.ds(WIDE, NARROW), NARROW),
    )
    for xr in (2, 1, 3):
        crossings[xr].wait_recv()
        for t in range(TILES):
            x_out[xr - 1, t] = (
                terms[0, xr, t].astype(F32) + pair_in[xr, t].astype(F32)
            ).astype(BF)
        if xr == 2:
            hops = {}
            for w in (0,):
                src, dst, _ = windows[w]
                hops[w, 0] = send(
                    x_out.at[1, src, GROUPS[0]], relay_in.at[0, dst],
                    rx_send.at[w, 0], rx_recv.at[w, 0], me.at(dx=1),
                )
                hops[w, 1] = send(
                    x_out.at[1, src, GROUPS[1]], relay_in.at[1, dst],
                    rx_send.at[w, 1], rx_recv.at[w, 1], me.at(dx=3),
                )

    def direct(w):
        src, dst, _ = windows[w]
        hops[w, 2] = send(
            x_out.at[0, src, GROUPS[1]], direct_in.at[0, dst],
            rx_send.at[w, 2], rx_recv.at[w, 2], me.at(dx=1),
        )
        hops[w, 3] = send(
            x_out.at[2, src, GROUPS[0]], direct_in.at[1, dst],
            rx_send.at[w, 3], rx_recv.at[w, 3], me.at(dx=3),
        )

    def relayed(w):
        src, dst, count = windows[w]
        for side, (xi, dx) in enumerate(((0, 1), (2, 3))):
            hops[w, side].wait_recv()
            relay_out[side, dst] = (
                x_out[xi, src, GROUPS[side]].astype(F32) + relay_in[side, dst].astype(F32)
            ).astype(BF)
            hops[w, 4 + side] = send(
                relay_out.at[side, dst], sum_in.at[side, dst],
                rx_send.at[w, 4 + side], rx_recv.at[w, 4 + side], me.at(dx=dx),
            )

    direct(0)
    src, dst, _ = windows[1]
    hops[1, 0] = send(
        x_out.at[1, src, GROUPS[0]], relay_in.at[0, dst],
        rx_send.at[1, 0], rx_recv.at[1, 0], me.at(dx=1),
    )
    hops[1, 1] = send(
        x_out.at[1, src, GROUPS[1]], relay_in.at[1, dst],
        rx_send.at[1, 1], rx_recv.at[1, 1], me.at(dx=3),
    )
    crossings[0].wait_recv()

    out = jnp.zeros((both, width), F32)
    step = 2 * chunk
    for zr in range(NZH):
        for half in range(2):
            at = pl.ds((zr * NX + 2 * half) * chunk, step)
            k_val = keys[zr, 2 * half : 2 * half + 2].reshape(step, width + rope)
            out += jnp.dot(p_ref[:, at], k_val[:, :width], preferred_element_type=F32)
    for h in range(heads):
        part = slice(h * rows, (h + 1) * rows)
        att_ref[:, h * value : (h + 1) * value] = jnp.dot(
            out[part].astype(BF), vu_ref[h], preferred_element_type=F32
        ).astype(BF)
    relayed(0)
    direct(1)
    joined = jnp.zeros((both, width), F32)
    joined_rotary = jnp.zeros((both, rope), F32)
    for zr in range(NZH):
        for half in range(2):
            at = pl.ds((zr * NX + 2 * half) * chunk, step)
            k_val = keys[zr, 2 * half : 2 * half + 2].reshape(step, width + rope)
            joined += jnp.dot(gs_ref[:, at], k_val[:, :width], preferred_element_type=F32)
            joined_rotary += jnp.dot(gs_ref[:, at], k_val[:, width:], preferred_element_type=F32)
    for h in range(heads):
        part = slice(h * rows, (h + 1) * rows)
        qg_ref[:, h * head_width : h * head_width + nope] = lax.dot_general(
            joined[part].astype(BF), ku_ref[h], NT, preferred_element_type=F32
        ).astype(BF)
        qg_ref[:, h * head_width + nope : (h + 1) * head_width] = joined_rotary[part].astype(BF)
    relayed(1)

    def summed(w, i):
        src, dst, _ = windows[w]
        tile = src.start + i
        at = dst.start + i
        base = terms[0, 0, tile].astype(F32) + pair_in[0, tile].astype(F32)
        first = base[:HALF] + sum_in[0, at].astype(F32) + direct_in[1, at].astype(F32)
        second = base[HALF:] + direct_in[0, at].astype(F32) + sum_in[1, at].astype(F32)
        return jnp.concatenate([first, second], axis=0).astype(BF)

    for i in range(2, 6):
        hops[0, i].wait_recv()
    for i in range(WIDE):
        y_far[:, i] = summed(0, i)
    ups = [
        send(
            y_far.at[slot], y_far_in.at[slot], ry_send.at[0, slot], ry_recv.at[0, slot],
            me.at(dy=SLOTS[slot], pair=1),
        )
        for slot in reversed(range(NY))
    ]
    for i in range(2, 6):
        hops[1, i].wait_recv()
    for i in range(NARROW):
        y_near[:, me.odd + i] = summed(1, i)
    y_near[:, 4 * (1 - me.odd)] = y_far[:, 4 * me.odd]
    ups += [
        send(
            y_near.at[slot], y_near_in.at[slot - 1], ry_send.at[1, slot], ry_recv.at[1, slot],
            me.at(dy=SLOTS[slot]),
        )
        for slot in reversed(range(1, NY))
    ]
    for up in ups:
        up.wait_recv()
    part = y_near[0].astype(F32)
    for i in range(NY):
        part += y_far_in[i].astype(F32)
    for i in range(NY - 1):
        part += y_near_in[i].astype(F32)
    w_ref[...] = part

    order = me.zl // 2
    rotary = w_ref[4 * (1 - me.odd)]
    z_out[0:2] = w_ref[pl.ds(2 + me.odd, 2)].astype(BF)
    z_out[2] = jnp.concatenate([rotary[:, rope:], rotary[:, :rope]], axis=1).astype(BF)
    ups = [
        send(
            z_out, z_far.at[order], rz_send.at[2 + i], rz_recv.at[2 + i], me.at(far=1, dzl=2 * i)
        )
        for i in range(3)
    ]
    z_own[order, 0:2] = w_ref[pl.ds(me.odd, 2)].astype(BF)
    z_own[order, 2] = rotary.astype(BF)
    ups += [
        send(
            z_own.at[order], z_own.at[order], rz_send.at[i], rz_recv.at[i], me.at(dzl=2 * i + 2)
        )
        for i in range(2)
    ]
    for up in ups:
        up.wait_recv()
    part = z_own[0].astype(F32)
    for i in range(1, 3):
        part += z_own[i].astype(F32)
    for i in range(3):
        part += z_far[i].astype(F32)
    final[me.odd, me.k, me.x] = part.astype(BF)
    place = final.at[me.odd, me.k, me.x]
    ups = [
        send(place, place, f_send.at[i], f_recv.at[i], me.at(**peer))
        for i, peer in enumerate(finals)
    ]
    for up in ups:
        up.wait_recv()
    for odd in range(2):
        for t in range(2):
            column = (2 * odd + t) * LANES
            grad_ref[:, column : column + LANES] = (
                final[odd, :, :, t].reshape(NC * NX * SR, LANES).astype(F32)
            )
    grad_ref[:, width:] = final[0, :, :, 2].reshape(NC * NX * SR, LANES)[:, :rope].astype(F32)
    for copy in pending:
        copy.wait_send()


def on_device(queries, latent, block_of, key_up, value_up, out_grad):
    rows, joined = latent.shape
    heads, nope, width = key_up.shape
    value = value_up.shape[2]
    rope = joined - width
    scale = 1.0 / math.sqrt(nope + rope)
    both = heads * rows
    total = NZH * NX * NC * NY * SR
    vmem = pl.BlockSpec(memory_space=pltpu.VMEM)
    dma = pltpu.SemaphoreType.DMA
    tile = (SR, LANES)
    return pl.pallas_call(
        functools.partial(kernel, scale, nope, rope, width, value, heads),
        out_shape=(
            jax.ShapeDtypeStruct(out_grad.shape, BF),
            jax.ShapeDtypeStruct(queries.shape, BF),
            jax.ShapeDtypeStruct((rows, joined), F32),
        ),
        in_specs=[pl.BlockSpec(memory_space=pltpu.SMEM)] + [vmem] * 5,
        out_specs=(vmem,) * 3,
        scratch_shapes=[
            pltpu.VMEM((NZH, NX, NC, NY, SR, joined), BF),
            pltpu.VMEM((both, rope), BF),
            pltpu.VMEM((both, width), BF),
            pltpu.VMEM((both, width), BF),
            pltpu.VMEM((both, total), F32),
            pltpu.VMEM((both, total), F32),
            pltpu.VMEM((both, total), BF),
            pltpu.VMEM((both, total), BF),
            pltpu.VMEM((NC, NX, TILES, NY, *tile), BF),
            pltpu.VMEM((NX, TILES, NY, *tile), BF),
            pltpu.VMEM((NX - 1, TILES, NY, *tile), BF),
            pltpu.VMEM((2, TILES, HALF, *tile), BF),
            pltpu.VMEM((2, TILES, HALF, *tile), BF),
            pltpu.VMEM((2, TILES, HALF, *tile), BF),
            pltpu.VMEM((2, TILES, HALF, *tile), BF),
            pltpu.VMEM((NY, WIDE, *tile), BF),
            pltpu.VMEM((NY, WIDE, *tile), BF),
            pltpu.VMEM((NY, WIDE, *tile), BF),
            pltpu.VMEM((NY - 1, WIDE, *tile), BF),
            pltpu.VMEM((WIDE, *tile), F32),
            pltpu.VMEM((3, 3, *tile), BF),
            pltpu.VMEM((3, *tile), BF),
            pltpu.VMEM((3, 3, *tile), BF),
            pltpu.VMEM((2, NC, NX, 3, *tile), BF),
            dma((2, NY - 1)), dma((2, NY - 1)),
            dma, dma,
            dma((2, 6)), dma((2, 6)),
            dma((2, NX)), dma((2, NX)),
            dma((NX,)), dma((NX,)),
            dma((2, 6)), dma((2, 6)),
            dma((2, NY)), dma((2, NY)),
            dma((5,)), dma((5,)),
            dma((15,)), dma((15,)),
        ],
        compiler_params=pltpu.CompilerParams(
            collective_id=0, has_side_effects=True, vmem_limit_bytes=48 * 1024 * 1024
        ),
    )(block_of, latent, queries, out_grad, key_up, value_up)


def solution(mesh):
    return jax.shard_map(
        on_device,
        mesh=mesh,
        in_specs=(
            P("ctx", "head"),
            P("ctx", None),
            P(),
            P("head", None, None),
            P("head", None, None),
            P("ctx", "head"),
        ),
        out_specs=(P("ctx", "head"), P("ctx", "head"), P("ctx", None)),
        check_vma=False,
    )
```

time: 707 us -> 83.7 us (0.12)
  waiting for transfers between devices: 631 us -> 0 us
  Pallas kernels: 0 us -> 76.9 us
  matrix products: 29.6 us -> 0 us
  between operations: 14.2 us -> 0.68 us
  local copies, waits for them, and re-layouts: 19.1 us -> 5.92 us
  starting transfers between devices: 9.78 us -> 0 us
    unnamed x3 -> x0, waiting for transfers between devices: 490 us -> none
    all_gather x1 -> x0, waiting for transfers between devices: 135 us -> none  [on_device(): all_latent = lax.all_gather(latent, 'ctx', axis=0, tiled=True)]
    pallas_call x0 -> x1, Pallas kernels: none -> 76.9 us  [on_device(): pl.pallas_call(functools.partial(kernel, scale, nope, rope, width, value,...]
    dot_general x9 -> x0, matrix products: 29.6 us -> none  [the longest x1 6.97 us: on_device(): jnp.einsum('htk,htw->kw', grad_scores, q_joined, preferred_element_type=j...]
    all_to_all x1 -> x0, starting transfers between devices: 9.7 us -> none  [sent_to_all(): return lax.all_to_all(copies, axis, split_axis=0, concat_axis=0, tiled=True)]
    reshape x2 -> x0, local copies, waits for them, and re-layouts: 7.23 us -> none  [the longest x1 7.12 us: on_device(): flat_terms = key_terms.reshape(total_rows * joined_width)]
  transfers between devices with their start and end apart: 3 -> 0, of which waited for: 3 -> 0; matrix products, arithmetic and copies ran while one was open for 2% -> 0% of each run, Pallas kernels for 0% -> 0%
where the time goes in v2:
time: 83.7 us; the launch traced here: 83.5 us
  Pallas kernels  76.9 us (92%)
  local copies, waits for them, and re-layouts  5.92 us (7%)
    pallas_call x1, Pallas kernels, on_device(): pl.pallas_call(functools.partial(kernel, scale, nope, rope, width, value,...  76.9 us
    unnamed x13, local copies, waits for them, and re-layouts  5.05 us

profile of v2, /device:TPU:1, one launch (start us, length us, event | category | flops | bytes accessed | tf_op | source)
XLA Modules:
  0.0 83.5 jit_solution(7428863473790794607)
XLA Ops:
  0.6 0.0 copy-start
  0.6 0.0 copy-start.4
  0.7 1.1 %copy.9.lat = bf16[128,576]{1,0:T(8,128)(2,1)S(1)} copy(bf16[128,576]{0,1:T(8,128)(2,1)} %param.7) | data formatting | bytes 294912 | tf_op args[1]
  1.8 0.0 copy-done
  1.8 0.0 copy-done.4
  1.8 0.0 copy-start.1
  1.8 0.9 %copy-done.1 = bf16[2,512,128]{2,1,0:T(8,128)(2,1)S(1)} copy-done((bf16[2,512,128]{2,1,0:T(8,128)(2,1)S(1)}, bf16[2,512,128]{2,1,0:T(8,128)(2,1)}, u32[]{:S(2)}) %copy-start.1) | copy-done | bytes 262168
  2.7 0.0 copy-start.2
  2.7 0.9 %copy-done.2 = bf16[128,384]{1,0:T(8,128)(2,1)S(1)} copy-done((bf16[128,384]{1,0:T(8,128)(2,1)S(1)}, bf16[128,384]{1,0:T(8,128)(2,1)}, u32[]{:S(2)}) %copy-start.2) | copy-done | bytes 98328
  3.6 0.0 copy-start.3
  3.6 0.8 %copy-done.3 = bf16[128,256]{1,0:T(8,128)(2,1)S(1)} copy-done((bf16[128,256]{1,0:T(8,128)(2,1)S(1)}, bf16[128,256]{1,0:T(8,128)(2,1)}, u32[]{:S(2)}) %copy-start.3) | copy-done | bytes 65560
  4.5 76.9 %shard_map.85 = (bf16[128,256]{1,0:T(8,128)(2,1)S(1)}, bf16[128,384]{1,0:T(8,128)(2,1)S(1)}, f32[128,576]{1,0:T(8,128)S(1)}) custom-call(s32[32]{0:T(128)S(1)} %copy-done.4, bf16[128,576]{1,0:T(8,128)(2,1)S(1)} %copy.9.lat, bf16[128,384]{1,0:T(8,128)(2,1)S(1)} %copy-done.2, bf16[128,256]{1,0:T(8,128)(2,1)S(1)} %copy-done.3, ...), custom_call_target="tpu_custom_call" | custom-call | tf_op jit(solution)/shard_map/pallas_call | solution.py:442
  81.3 0.9 %copy.10 = f32[128,576]{0,1:T(8,128)} copy(f32[128,576]{1,0:T(8,128)S(1)} %get-tuple-element.5) | data formatting | bytes 589824 | tf_op jit(solution)/shard_map/pallas_call | solution.py:442
  82.2 0.6 copy.13
  82.8 0.6 copy.14
Async XLA Ops:
  0.6 1.1 %copy-start = (bf16[2,128,512]{2,1,0:T(8,128)(2,1)S(1)}, bf16[2,128,512]{2,1,0:T(8,128)(2,1)}, u32[]{:S(2)}) copy-start(bf16[2,128,512]{2,1,0:T(8,128)(2,1)} %ku_ref.1) | copy-start | bytes 786436
  0.6 1.1 %copy-start.4 = (s32[32]{0:T(128)S(1)}, s32[32]{0:T(128)}, u32[]{:S(2)}) copy-start(s32[32]{0:T(128)} %blocks.1) | copy-start | bytes 388
  1.8 1.0 %copy-start.1 = (bf16[2,512,128]{2,1,0:T(8,128)(2,1)S(1)}, bf16[2,512,128]{2,1,0:T(8,128)(2,1)}, u32[]{:S(2)}) copy-start(bf16[2,512,128]{2,1,0:T(8,128)(2,1)} %vu_ref.1) | copy-start | bytes 786436
  2.7 0.9 %copy-start.2 = (bf16[128,384]{1,0:T(8,128)(2,1)S(1)}, bf16[128,384]{1,0:T(8,128)(2,1)}, u32[]{:S(2)}) copy-start(bf16[128,384]{1,0:T(8,128)(2,1)} %q_ref.1) | copy-start | bytes 294916
  3.6 0.8 %copy-start.3 = (bf16[128,256]{1,0:T(8,128)(2,1)S(1)}, bf16[128,256]{1,0:T(8,128)(2,1)}, u32[]{:S(2)}) copy-start(bf16[128,256]{1,0:T(8,128)(2,1)} %g_ref.1) | copy-start | bytes 196612

commit v3 on v2

--- a/solution.py
+++ b/solution.py
@@ -35,6 +35,7 @@
         self.zl = lax.rem(h // NC, NZL)
         self.x = h // (NC * NZL)
         self.odd = lax.rem(self.zl, 2)
+        self.side = lax.rem(self.zl + self.zh, 2)
 
     def at(self, dy=0, dx=0, dk=0, pair=0, dzl=0, far=0, mirror=False):
         zh = 1 - self.zh if far else self.zh
@@ -53,11 +54,12 @@
 
 def kernel(
     scale, nope, rope, width, value, heads,
-    blocks, lat, q_ref, g_ref, ku_ref, vu_ref,
+    blocks, lat_hbm, q_hbm, g_hbm, ku_hbm, vu_hbm,
     att_ref, qg_ref, grad_ref,
+    final, lat_t, lat, q_ref, g_ref, ku_ref, vu_ref, in_sem,
     keys, qr_ref, ql_ref, gl_ref, s_ref, gp_ref, p_ref, gs_ref,
     terms, pair_in, x_out, relay_in, direct_in, relay_out, sum_in,
-    y_far, y_near, y_far_in, y_near_in, w_ref, z_own, z_out, z_far, final,
+    y_far, y_near, y_far_in, y_near_in, w_ref, z_own, z_out, z_far,
     y_send, y_recv, m_send, m_recv, x_send, x_recv, d_send, d_recv,
     p_send, p_recv, rx_send, rx_recv, ry_send, ry_recv, rz_send, rz_recv, f_send, f_recv,
 ):
@@ -85,13 +87,27 @@
         [dict(dy=d) for d in range(1, NY)]
         + [dict(dy=d, pair=1) for d in range(1, NY)]
         + finals
-        + [dict(dzl=2), dict(dzl=4), dict(far=1), dict(far=1, dzl=2), dict(far=1, dzl=4)]
-        + [dict(far=1, mirror=True)]
+        + [dict(dzl=2), dict(dzl=4)]
+        + [dict(far=1, mirror=True, dzl=d) for d in (0, 2, 4)]
     )
     barrier = pltpu.get_barrier_semaphore()
     for peer in peers:
         pl.semaphore_signal(barrier, inc=1, device_id=me.at(**peer), device_id_type=MESH)
 
+    loads = [
+        pltpu.make_async_copy(src, dst, in_sem.at[i])
+        for i, (src, dst) in enumerate(
+            ((lat_hbm, lat_t), (q_hbm, q_ref), (ku_hbm, ku_ref), (g_hbm, g_ref), (vu_hbm, vu_ref))
+        )
+    ]
+    for load in loads:
+        load.start()
+    loads[0].wait()
+    for t in range(0, width, LANES):
+        lat[:, t : t + LANES] = lat_t[t : t + LANES, :].T
+    lat[:, width:] = lat_t[width:, :].T
+    for load in loads[1:]:
+        load.wait()
     for h in range(heads):
         at = pl.ds(h * rows, rows)
         qn = q_ref[:, h * head_width : h * head_width + nope]
@@ -135,9 +151,9 @@
             for d in (7, 1, 6, 2, 5, 3, 4)
         }
 
-    def x_copy(zr, i, src_x, dst_x, group, dx):
+    def x_copy(zr, i, src_x, dst_x, part, dx):
         return send(
-            keys.at[zr, src_x, 0, GROUPS[group]], keys.at[zr, dst_x, 0, GROUPS[group]],
+            keys.at[zr, src_x, 0, part], keys.at[zr, dst_x, 0, part],
             x_send.at[zr, i], x_recv.at[zr, i], me.at(dx=dx),
         )
 
@@ -147,35 +163,30 @@
             me.at(dk=1),
         )
 
-    def spread(zr, arrivals):
-        for j in SLOTS[1:HALF]:
-            arrivals[j].wait_recv()
-        a_right = x_copy(zr, 0, 0, 3, 0, 1)
-        a_left = x_copy(zr, 1, 0, 1, 0, 3)
-        for j in SLOTS[HALF:]:
-            arrivals[j].wait_recv()
-        b_left = x_copy(zr, 2, 0, 1, 1, 3)
-        b_right = x_copy(zr, 3, 0, 3, 1, 1)
-        return a_right, a_left, b_left, b_right, cross(zr, 0)
-
-    def forward(zr, moves):
-        a_right, a_left, b_left, b_right, _ = moves
-        a_right.wait_recv()
-        relay_a = x_copy(zr, 4, 3, 2, 0, 1)
-        b_left.wait_recv()
-        relay_b = x_copy(zr, 5, 1, 2, 1, 3)
-        b_right.wait_recv()
-        from_left = cross(zr, 3)
-        a_left.wait_recv()
-        from_right = cross(zr, 1)
-        return relay_a, relay_b, from_left, from_right
-
-    def close(zr, relays):
-        relays[0].wait_recv()
-        relays[1].wait_recv()
+    def spread(zr, group, arrivals):
+        for j in SLOTS[group * HALF : (group + 1) * HALF]:
+            if j:
+                arrivals[j].wait_recv()
+        part = GROUPS[group]
+        return (
+            x_copy(zr, 4 * group, 0, 3, part, 1),
+            x_copy(zr, 4 * group + 1, 0, 1, part, 3),
+        )
+
+    def relay(zr, group, moves):
+        start = group * HALF
+        moves[0].wait_recv()
+        right = x_copy(zr, 4 * group + 2, 3, 2, pl.ds(start, HALF // 2), 1)
+        moves[1].wait_recv()
+        left = x_copy(zr, 4 * group + 3, 1, 2, pl.ds(start + HALF // 2, HALF // 2), 3)
+        return right, left
+
+    def close(zr, *relays):
+        for copy in relays:
+            copy.wait_recv()
         return cross(zr, 2)
 
-    maxima = []
+    stats = {}
 
     def score(zr, xr, arrived):
         arrived.wait_recv()
@@ -190,48 +201,57 @@
         part = jnp.concatenate(
             [jnp.where(seen, part[h * rows : (h + 1) * rows], -1e30) for h in range(heads)], axis=0
         )
-        s_ref[:, at] = part
-        maxima.append(jnp.max(part, axis=1, keepdims=True))
-        gp_ref[:, at] = lax.dot_general(
-            gl_ref[...], k_val[:, :width], NT, preferred_element_type=F32
+        high = jnp.max(part, axis=1, keepdims=True)
+        expo = jnp.exp(part - high)
+        back = lax.dot_general(gl_ref[...], k_val[:, :width], NT, preferred_element_type=F32)
+        s_ref[:, at] = expo
+        gp_ref[:, at] = back
+        stats[zr, xr] = (
+            high,
+            jnp.sum(expo, axis=1, keepdims=True),
+            jnp.sum(expo * back, axis=1, keepdims=True),
         )
 
     near = along_y(0, own)
-    near_moves = spread(0, near)
+    near_a = spread(0, 0, near)
     to_mirror.wait_recv()
     far = along_y(1, keys.at[1, 0, 0, 0])
-    near_relays = forward(0, near_moves)
-    score(0, 0, near_moves[4])
-    far_moves = spread(1, far)
-    near_last = close(0, near_relays)
-    score(0, 3, near_relays[2])
-    score(0, 1, near_relays[3])
-    far_relays = forward(1, far_moves)
-    score(0, 2, near_last)
-    score(1, 0, far_moves[4])
-    far_last = close(1, far_relays)
-    score(1, 3, far_relays[2])
-    score(1, 1, far_relays[3])
-    score(1, 2, far_last)
-
-    low = functools.reduce(jnp.maximum, maxima)
-    total = jnp.zeros((both, 1), F32)
-    delta = jnp.zeros((both, 1), F32)
-    for i in range(NZH * NX):
-        at = pl.ds(i * chunk, chunk)
-        expo = jnp.exp(s_ref[:, at] - low)
-        s_ref[:, at] = expo
-        total += jnp.sum(expo, axis=1, keepdims=True)
-        delta += jnp.sum(expo * gp_ref[:, at], axis=1, keepdims=True)
-    inverse = 1.0 / total
-    delta = delta * inverse
+    near_b = spread(0, 1, near)
+    across = {(0, 0): cross(0, 0)}
+    near_relay_a = relay(0, 0, near_a)
+    far_a = spread(1, 0, far)
+    near_relay_b = relay(0, 1, near_b)
+    across[0, 3] = cross(0, 3)
+    across[0, 1] = cross(0, 1)
+    score(0, 0, across[0, 0])
+    far_b = spread(1, 1, far)
+    across[1, 0] = cross(1, 0)
+    across[0, 2] = close(0, *near_relay_a, *near_relay_b)
+    far_relay_a = relay(1, 0, far_a)
+    score(0, 3, across[0, 3])
+    score(0, 1, across[0, 1])
+    far_relay_b = relay(1, 1, far_b)
+    across[1, 3] = cross(1, 3)
+    across[1, 1] = cross(1, 1)
+    score(0, 2, across[0, 2])
+    score(1, 0, across[1, 0])
+    across[1, 2] = close(1, *far_relay_a, *far_relay_b)
+    score(1, 3, across[1, 3])
+    score(1, 1, across[1, 1])
+    score(1, 2, across[1, 2])
+
+    top = functools.reduce(jnp.maximum, [high for high, _, _ in stats.values()])
+    factor = {i: jnp.exp(high - top) for i, (high, _, _) in stats.items()}
+    inverse = 1.0 / sum(factor[i] * total for i, (_, total, _) in stats.items())
+    delta = sum(factor[i] * dot for i, (_, _, dot) in stats.items()) * inverse
 
     crossings = {}
-    for xr in (2, 1, 3, 0):
+
+    def make_terms(xr):
         rotary = []
         for zr in range(NZH):
             at = pl.ds((zr * NX + xr) * chunk, chunk)
-            probs = s_ref[:, at] * inverse
+            probs = s_ref[:, at] * (factor[zr, xr] * inverse)
             probs_low = probs.astype(BF)
             grads = (probs * (gp_ref[:, at] - delta) * scale).astype(BF)
             p_ref[:, at] = probs_low
@@ -256,27 +276,25 @@
         )
 
     windows = (
-        (pl.ds(4 * (1 - me.odd), WIDE), pl.ds(0, WIDE), WIDE),
-        (pl.ds(5 * me.odd, NARROW), pl.ds(WIDE, NARROW), NARROW),
+        (pl.ds(4 * (1 - me.side), WIDE), pl.ds(0, WIDE), WIDE),
+        (pl.ds(5 * me.side, NARROW), pl.ds(WIDE, NARROW), NARROW),
     )
-    for xr in (2, 1, 3):
+    hops = {}
+
+    def pair_sum(xr):
         crossings[xr].wait_recv()
         for t in range(TILES):
             x_out[xr - 1, t] = (
                 terms[0, xr, t].astype(F32) + pair_in[xr, t].astype(F32)
             ).astype(BF)
-        if xr == 2:
-            hops = {}
-            for w in (0,):
-                src, dst, _ = windows[w]
-                hops[w, 0] = send(
-                    x_out.at[1, src, GROUPS[0]], relay_in.at[0, dst],
-                    rx_send.at[w, 0], rx_recv.at[w, 0], me.at(dx=1),
-                )
-                hops[w, 1] = send(
-                    x_out.at[1, src, GROUPS[1]], relay_in.at[1, dst],
-                    rx_send.at[w, 1], rx_recv.at[w, 1], me.at(dx=3),
-                )
+
+    def opposite(w):
+        src, dst, _ = windows[w]
+        for side, dx in enumerate((1, 3)):
+            hops[w, side] = send(
+                x_out.at[1, src, GROUPS[side]], relay_in.at[side, dst],
+                rx_send.at[w, side], rx_recv.at[w, side], me.at(dx=dx),
+            )
 
     def direct(w):
         src, dst, _ = windows[w]
@@ -301,16 +319,16 @@
                 rx_send.at[w, 4 + side], rx_recv.at[w, 4 + side], me.at(dx=dx),
             )
 
+    make_terms(2)
+    make_terms(1)
+    make_terms(3)
+    pair_sum(2)
+    opposite(0)
+    pair_sum(1)
+    make_terms(0)
+    pair_sum(3)
     direct(0)
-    src, dst, _ = windows[1]
-    hops[1, 0] = send(
-        x_out.at[1, src, GROUPS[0]], relay_in.at[0, dst],
-        rx_send.at[1, 0], rx_recv.at[1, 0], me.at(dx=1),
-    )
-    hops[1, 1] = send(
-        x_out.at[1, src, GROUPS[1]], relay_in.at[1, dst],
-        rx_send.at[1, 1], rx_recv.at[1, 1], me.at(dx=3),
-    )
+    opposite(1)
     crossings[0].wait_recv()
 
     out = jnp.zeros((both, width), F32)
@@ -366,8 +384,8 @@
     for i in range(2, 6):
         hops[1, i].wait_recv()
     for i in range(NARROW):
-        y_near[:, me.odd + i] = summed(1, i)
-    y_near[:, 4 * (1 - me.odd)] = y_far[:, 4 * me.odd]
+        y_near[:, me.side + i] = summed(1, i)
+    y_near[:, 4 * (1 - me.side)] = y_far[:, 4 * me.side]
     ups += [
         send(
             y_near.at[slot], y_near_in.at[slot - 1], ry_send.at[1, slot], ry_recv.at[1, slot],
@@ -385,16 +403,16 @@
     w_ref[...] = part
 
     order = me.zl // 2
-    rotary = w_ref[4 * (1 - me.odd)]
-    z_out[0:2] = w_ref[pl.ds(2 + me.odd, 2)].astype(BF)
+    rotary = w_ref[4 * (1 - me.side)]
+    z_out[0:2] = w_ref[pl.ds(2 + me.side, 2)].astype(BF)
     z_out[2] = jnp.concatenate([rotary[:, rope:], rotary[:, :rope]], axis=1).astype(BF)
     ups = [
         send(
-            z_out, z_far.at[order], rz_send.at[2 + i], rz_recv.at[2 + i], me.at(far=1, dzl=2 * i)
+            z_out, z_far.at[order], rz_send.at[2 + i], rz_recv.at[2 + i], me.at(far=1, mirror=True, dzl=2 * i)
         )
         for i in range(3)
     ]
-    z_own[order, 0:2] = w_ref[pl.ds(me.odd, 2)].astype(BF)
+    z_own[order, 0:2] = w_ref[pl.ds(me.side, 2)].astype(BF)
     z_own[order, 2] = rotary.astype(BF)
     ups += [
         send(
@@ -409,21 +427,19 @@
         part += z_own[i].astype(F32)
     for i in range(3):
         part += z_far[i].astype(F32)
-    final[me.odd, me.k, me.x] = part.astype(BF)
-    place = final.at[me.odd, me.k, me.x]
+    final[me.side, me.k, me.x] = part.astype(BF)
+    place = final.at[me.side, me.k, me.x]
     ups = [
         send(place, place, f_send.at[i], f_recv.at[i], me.at(**peer))
         for i, peer in enumerate(finals)
     ]
     for up in ups:
         up.wait_recv()
-    for odd in range(2):
+    for side in range(2):
         for t in range(2):
-            column = (2 * odd + t) * LANES
-            grad_ref[:, column : column + LANES] = (
-                final[odd, :, :, t].reshape(NC * NX * SR, LANES).astype(F32)
-            )
-    grad_ref[:, width:] = final[0, :, :, 2].reshape(NC * NX * SR, LANES)[:, :rope].astype(F32)
+            at = (2 * side + t) * LANES
+            grad_ref[at : at + LANES, :] = final[side, :, :, t].reshape(rows, LANES).astype(F32).T
+    grad_ref[width:, :] = final[0, :, :, 2].reshape(rows, LANES).astype(F32).T[:rope]
     for copy in pending:
         copy.wait_send()
 
@@ -437,18 +453,27 @@
     both = heads * rows
     total = NZH * NX * NC * NY * SR
     vmem = pl.BlockSpec(memory_space=pltpu.VMEM)
+    anywhere = pl.BlockSpec(memory_space=pltpu.HBM)
     dma = pltpu.SemaphoreType.DMA
     tile = (SR, LANES)
-    return pl.pallas_call(
+    attended, query_grad, grad = pl.pallas_call(
         functools.partial(kernel, scale, nope, rope, width, value, heads),
         out_shape=(
-            jax.ShapeDtypeStruct(out_grad.shape, BF),
-            jax.ShapeDtypeStruct(queries.shape, BF),
-            jax.ShapeDtypeStruct((rows, joined), F32),
+            pltpu.VMEM(out_grad.shape, BF),
+            pltpu.VMEM(queries.shape, BF),
+            pltpu.VMEM((joined, rows), F32),
         ),
-        in_specs=[pl.BlockSpec(memory_space=pltpu.SMEM)] + [vmem] * 5,
+        in_specs=[pl.BlockSpec(memory_space=pltpu.SMEM)] + [anywhere] * 5,
         out_specs=(vmem,) * 3,
         scratch_shapes=[
+            pltpu.VMEM((2, NC, NX, 3, *tile), BF),
+            pltpu.VMEM((joined, rows), BF),
+            pltpu.VMEM((rows, joined), BF),
+            pltpu.VMEM(queries.shape, BF),
+            pltpu.VMEM(out_grad.shape, BF),
+            pltpu.VMEM(key_up.shape, BF),
+            pltpu.VMEM(value_up.shape, BF),
+            dma((5,)),
             pltpu.VMEM((NZH, NX, NC, NY, SR, joined), BF),
             pltpu.VMEM((both, rope), BF),
             pltpu.VMEM((both, width), BF),
@@ -472,10 +497,9 @@
             pltpu.VMEM((3, 3, *tile), BF),
             pltpu.VMEM((3, *tile), BF),
             pltpu.VMEM((3, 3, *tile), BF),
-            pltpu.VMEM((2, NC, NX, 3, *tile), BF),
             dma((2, NY - 1)), dma((2, NY - 1)),
             dma, dma,
-            dma((2, 6)), dma((2, 6)),
+            dma((2, 8)), dma((2, 8)),
             dma((2, NX)), dma((2, NX)),
             dma((NX,)), dma((NX,)),
             dma((2, 6)), dma((2, 6)),
@@ -484,9 +508,10 @@
             dma((15,)), dma((15,)),
         ],
         compiler_params=pltpu.CompilerParams(
-            collective_id=0, has_side_effects=True, vmem_limit_bytes=48 * 1024 * 1024
+            collective_id=0, has_side_effects=True, vmem_limit_bytes=56 * 1024 * 1024
         ),
-    )(block_of, latent, queries, out_grad, key_up, value_up)
+    )(block_of, latent.T, queries, out_grad, key_up, value_up)
+    return attended, query_grad, grad.T
 
 
 def solution(mesh):

time: 83.7 us -> 78 us (0.932)
  local copies, waits for them, and re-layouts: 5.92 us -> 1.99 us
  Pallas kernels: 76.9 us -> 75.2 us
    unnamed x13 -> x3, local copies, waits for them, and re-layouts: 5.05 us -> 1.99 us
    pallas_call x1, Pallas kernels: 76.9 us -> 75.2 us  [on_device(): pl.pallas_call(functools.partial(kernel, scale, nope, rope, width, value,...]
    pallas_call x1 -> x0, local copies, waits for them, and re-layouts: 0.87 us -> none  [on_device(): pl.pallas_call(functools.partial(kernel, scale, nope, rope, width, value,...]
where the time goes in v3:
time: 78 us; the launch traced here: 77.8 us
  Pallas kernels  75.2 us (96%)
  local copies, waits for them, and re-layouts  1.99 us (3%)
    pallas_call x1, Pallas kernels, on_device(): pl.pallas_call(functools.partial(kernel, scale, nope, rope, width, value,...  75.2 us
    unnamed x3, local copies, waits for them, and re-layouts  1.99 us

profile of v3, /device:TPU:1, one launch (start us, length us, event | category | flops | bytes accessed | tf_op | source)
XLA Modules:
  0.0 77.8 jit_solution(12073020503014233192)
XLA Ops:
  0.6 75.2 %shard_map.85 = (bf16[128,256]{1,0:T(8,128)(2,1)S(1)}, bf16[128,384]{1,0:T(8,128)(2,1)S(1)}, f32[576,128]{1,0:T(8,128)S(1)}) custom-call(s32[32]{0:T(128)} %blocks.1, bf16[576,128]{1,0:T(8,128)(2,1)} %bitcast.3, bf16[128,384]{1,0:T(8,128)(2,1)} %q_hbm.1, bf16[128,256]{1,0:T(8,128)(2,1)} %g_hbm.1, bf16[2,128,512]{2,1,0:T(8,128)(2,1)} %ku_hbm.1, ...), custom_call_target="tpu_custom_call" | custom-call | tf_op jit(solution)/shard_map/pallas_call | solution.py:459
  75.9 0.6 copy.12
  76.5 0.6 copy.13
  77.1 0.7 copy.14

commit v4 on v3

--- a/solution.py
+++ b/solution.py
@@ -54,9 +54,9 @@
 
 def kernel(
     scale, nope, rope, width, value, heads,
-    blocks, lat_hbm, q_hbm, g_hbm, ku_hbm, vu_hbm,
-    att_ref, qg_ref, grad_ref,
-    final, lat_t, lat, q_ref, g_ref, ku_ref, vu_ref, in_sem,
+    blocks_hbm, lat_hbm, q_hbm, g_hbm, ku_hbm, vu_hbm,
+    att_ref, qg_ref, final,
+    blocks, lat_t, lat, q_ref, g_ref, ku_ref, vu_ref, in_sem,
     keys, qr_ref, ql_ref, gl_ref, s_ref, gp_ref, p_ref, gs_ref,
     terms, pair_in, x_out, relay_in, direct_in, relay_out, sum_in,
     y_far, y_near, y_far_in, y_near_in, w_ref, z_own, z_out, z_far,
@@ -97,7 +97,10 @@
     loads = [
         pltpu.make_async_copy(src, dst, in_sem.at[i])
         for i, (src, dst) in enumerate(
-            ((lat_hbm, lat_t), (q_hbm, q_ref), (ku_hbm, ku_ref), (g_hbm, g_ref), (vu_hbm, vu_ref))
+            (
+                (lat_hbm, lat_t), (q_hbm, q_ref), (ku_hbm, ku_ref), (g_hbm, g_ref),
+                (vu_hbm, vu_ref), (blocks_hbm, blocks),
+            )
         )
     ]
     for load in loads:
@@ -106,6 +109,86 @@
     for t in range(0, width, LANES):
         lat[:, t : t + LANES] = lat_t[t : t + LANES, :].T
     lat[:, width:] = lat_t[width:, :].T
+    mine = pl.ds(pl.multiple_of((me.k * NX + me.x) * SR, SR), SR)
+    keys[0, 0, 0, 0] = lat[mine, :]
+
+    pl.semaphore_wait(barrier, len(peers))
+
+    own = lat.at[mine, :]
+    to_mirror = send(own, keys.at[1, 0, 0, 0], m_send, m_recv, me.at(far=1, mirror=True))
+
+    def along_y(zr, src):
+        return {
+            NY - d: send(
+                src, keys.at[zr, 0, 0, SLOT_OF[NY - d]],
+                y_send.at[zr, d - 1], y_recv.at[zr, d - 1], me.at(dy=d),
+            )
+            for d in (7, 1, 6, 2, 5, 3, 4)
+        }
+
+    def x_copy(zr, i, src_x, dst_x, part, dx):
+        return send(
+            keys.at[zr, src_x, 0, part], keys.at[zr, dst_x, 0, part],
+            x_send.at[zr, i], x_recv.at[zr, i], me.at(dx=dx),
+        )
+
+    def cross(zr, xr):
+        return send(
+            keys.at[zr, xr, 0], keys.at[zr, xr, 1], d_send.at[zr, xr], d_recv.at[zr, xr],
+            me.at(dk=1),
+        )
+
+    def spread(zr, group, arrivals):
+        for j in SLOTS[group * HALF : (group + 1) * HALF]:
+            if j:
+                arrivals[j].wait_recv()
+        part = GROUPS[group]
+        return (
+            x_copy(zr, 4 * group, 0, 3, part, 1),
+            x_copy(zr, 4 * group + 1, 0, 1, part, 3),
+        )
+
+    def relay(zr, group, moves):
+        start = group * HALF
+        moves[0].wait_recv()
+        right = x_copy(zr, 4 * group + 2, 3, 2, pl.ds(start, HALF // 2), 1)
+        moves[1].wait_recv()
+        left = x_copy(zr, 4 * group + 3, 1, 2, pl.ds(start + HALF // 2, HALF // 2), 3)
+        return right, left
+
+    def close(zr, *relays):
+        for copy in relays:
+            copy.wait_recv()
+        return cross(zr, 2)
+
+    stats = {}
+
+    def score(zr, xr, arrived):
+        arrived.wait_recv()
+        at = pl.ds((zr * NX + xr) * chunk, chunk)
+        k_val = keys[zr, xr].reshape(chunk, width + rope)
+        part = lax.dot_general(
+            ql_ref[...], k_val[:, :width], NT, preferred_element_type=F32
+        ) + lax.dot_general(qr_ref[...], k_val[:, width:], NT, preferred_element_type=F32)
+        key_pos = starts[zr] + lax.rem(me.x + xr, NX) * SR
+        seen = key_pos <= my_pos
+        part = part * scale
+        part = jnp.concatenate(
+            [jnp.where(seen, part[h * rows : (h + 1) * rows], -1e30) for h in range(heads)], axis=0
+        )
+        high = jnp.max(part, axis=1, keepdims=True)
+        expo = jnp.exp(part - high)
+        back = lax.dot_general(gl_ref[...], k_val[:, :width], NT, preferred_element_type=F32)
+        s_ref[:, at] = expo
+        gp_ref[:, at] = back
+        stats[zr, xr] = (
+            high,
+            jnp.sum(expo, axis=1, keepdims=True),
+            jnp.sum(expo * back, axis=1, keepdims=True),
+        )
+
+    near = along_y(0, own)
+
     for load in loads[1:]:
         load.wait()
     for h in range(heads):
@@ -134,85 +217,7 @@
                     lane // SR == kr * NY + slot, blocks[2 * owner + k] * block, start
                 )
         starts.append(start + lax.rem(lane, SR))
-    mine = pl.ds(pl.multiple_of((me.k * NX + me.x) * SR, SR), SR)
-    keys[0, 0, 0, 0] = lat[mine, :]
-
-    pl.semaphore_wait(barrier, len(peers))
-
-    own = lat.at[mine, :]
-    to_mirror = send(own, keys.at[1, 0, 0, 0], m_send, m_recv, me.at(far=1, mirror=True))
-
-    def along_y(zr, src):
-        return {
-            NY - d: send(
-                src, keys.at[zr, 0, 0, SLOT_OF[NY - d]],
-                y_send.at[zr, d - 1], y_recv.at[zr, d - 1], me.at(dy=d),
-            )
-            for d in (7, 1, 6, 2, 5, 3, 4)
-        }
-
-    def x_copy(zr, i, src_x, dst_x, part, dx):
-        return send(
-            keys.at[zr, src_x, 0, part], keys.at[zr, dst_x, 0, part],
-            x_send.at[zr, i], x_recv.at[zr, i], me.at(dx=dx),
-        )
-
-    def cross(zr, xr):
-        return send(
-            keys.at[zr, xr, 0], keys.at[zr, xr, 1], d_send.at[zr, xr], d_recv.at[zr, xr],
-            me.at(dk=1),
-        )
-
-    def spread(zr, group, arrivals):
-        for j in SLOTS[group * HALF : (group + 1) * HALF]:
-            if j:
-                arrivals[j].wait_recv()
-        part = GROUPS[group]
-        return (
-            x_copy(zr, 4 * group, 0, 3, part, 1),
-            x_copy(zr, 4 * group + 1, 0, 1, part, 3),
-        )
-
-    def relay(zr, group, moves):
-        start = group * HALF
-        moves[0].wait_recv()
-        right = x_copy(zr, 4 * group + 2, 3, 2, pl.ds(start, HALF // 2), 1)
-        moves[1].wait_recv()
-        left = x_copy(zr, 4 * group + 3, 1, 2, pl.ds(start + HALF // 2, HALF // 2), 3)
-        return right, left
-
-    def close(zr, *relays):
-        for copy in relays:
-            copy.wait_recv()
-        return cross(zr, 2)
-
-    stats = {}
-
-    def score(zr, xr, arrived):
-        arrived.wait_recv()
-        at = pl.ds((zr * NX + xr) * chunk, chunk)
-        k_val = keys[zr, xr].reshape(chunk, width + rope)
-        part = lax.dot_general(
-            ql_ref[...], k_val[:, :width], NT, preferred_element_type=F32
-        ) + lax.dot_general(qr_ref[...], k_val[:, width:], NT, preferred_element_type=F32)
-        key_pos = starts[zr] + lax.rem(me.x + xr, NX) * SR
-        seen = key_pos <= my_pos
-        part = part * scale
-        part = jnp.concatenate(
-            [jnp.where(seen, part[h * rows : (h + 1) * rows], -1e30) for h in range(heads)], axis=0
-        )
-        high = jnp.max(part, axis=1, keepdims=True)
-        expo = jnp.exp(part - high)
-        back = lax.dot_general(gl_ref[...], k_val[:, :width], NT, preferred_element_type=F32)
-        s_ref[:, at] = expo
-        gp_ref[:, at] = back
-        stats[zr, xr] = (
-            high,
-            jnp.sum(expo, axis=1, keepdims=True),
-            jnp.sum(expo * back, axis=1, keepdims=True),
-        )
-
-    near = along_y(0, own)
+
     near_a = spread(0, 0, near)
     to_mirror.wait_recv()
     far = along_y(1, keys.at[1, 0, 0, 0])
@@ -433,15 +438,28 @@
         send(place, place, f_send.at[i], f_recv.at[i], me.at(**peer))
         for i, peer in enumerate(finals)
     ]
+    for copy in pending[: -len(finals)]:
+        copy.wait_send()
     for up in ups:
-        up.wait_recv()
+        up.wait()
+
+
+def write_kernel(rope, att, qg, final, att_hbm, qg_hbm, grad_hbm, grad, sem):
+    copies = [
+        pltpu.make_async_copy(src, dst, sem.at[i])
+        for i, (src, dst) in enumerate(((att, att_hbm), (qg, qg_hbm), (grad, grad_hbm)))
+    ]
+    copies[0].start()
+    copies[1].start()
+    width, rows = grad.shape
     for side in range(2):
         for t in range(2):
             at = (2 * side + t) * LANES
-            grad_ref[at : at + LANES, :] = final[side, :, :, t].reshape(rows, LANES).astype(F32).T
-    grad_ref[width:, :] = final[0, :, :, 2].reshape(rows, LANES).astype(F32).T[:rope]
-    for copy in pending:
-        copy.wait_send()
+            grad[at : at + LANES, :] = final[side, :, :, t].reshape(rows, LANES).astype(F32).T
+    grad[width - rope :, :] = final[0, :, :, 2].reshape(rows, LANES).astype(F32).T[:rope]
+    copies[2].start()
+    for copy in copies:
+        copy.wait()
 
 
 def on_device(queries, latent, block_of, key_up, value_up, out_grad):
@@ -453,27 +471,27 @@
     both = heads * rows
     total = NZH * NX * NC * NY * SR
     vmem = pl.BlockSpec(memory_space=pltpu.VMEM)
-    anywhere = pl.BlockSpec(memory_space=pltpu.HBM)
+    anywhere = pl.BlockSpec(memory_space=pl.ANY)
     dma = pltpu.SemaphoreType.DMA
     tile = (SR, LANES)
-    attended, query_grad, grad = pl.pallas_call(
+    results = pl.pallas_call(
         functools.partial(kernel, scale, nope, rope, width, value, heads),
         out_shape=(
             pltpu.VMEM(out_grad.shape, BF),
             pltpu.VMEM(queries.shape, BF),
-            pltpu.VMEM((joined, rows), F32),
+            pltpu.VMEM((2, NC, NX, 3, *tile), BF),
         ),
-        in_specs=[pl.BlockSpec(memory_space=pltpu.SMEM)] + [anywhere] * 5,
+        in_specs=[anywhere] * 6,
         out_specs=(vmem,) * 3,
         scratch_shapes=[
-            pltpu.VMEM((2, NC, NX, 3, *tile), BF),
+            pltpu.SMEM(block_of.shape, jnp.int32),
             pltpu.VMEM((joined, rows), BF),
             pltpu.VMEM((rows, joined), BF),
             pltpu.VMEM(queries.shape, BF),
             pltpu.VMEM(out_grad.shape, BF),
             pltpu.VMEM(key_up.shape, BF),
             pltpu.VMEM(value_up.shape, BF),
-            dma((5,)),
+            dma((6,)),
             pltpu.VMEM((NZH, NX, NC, NY, SR, joined), BF),
             pltpu.VMEM((both, rope), BF),
             pltpu.VMEM((both, width), BF),
@@ -511,6 +529,18 @@
             collective_id=0, has_side_effects=True, vmem_limit_bytes=56 * 1024 * 1024
         ),
     )(block_of, latent.T, queries, out_grad, key_up, value_up)
+
+    attended, query_grad, grad = pl.pallas_call(
+        functools.partial(write_kernel, rope),
+        out_shape=(
+            jax.ShapeDtypeStruct(out_grad.shape, BF),
+            jax.ShapeDtypeStruct(queries.shape, BF),
+            jax.ShapeDtypeStruct((joined, rows), F32),
+        ),
+        in_specs=[vmem] * 3,
+        out_specs=(anywhere,) * 3,
+        scratch_shapes=[pltpu.VMEM((joined, rows), F32), dma((3,))],
+    )(*(pltpu.with_memory_space_constraint(a, pltpu.VMEM) for a in results))
     return attended, query_grad, grad.T
 
 

time: 78 us -> 76 us (0.974)
  local copies, waits for them, and re-layouts: 1.99 us -> 0 us
    unnamed x3 -> x0, local copies, waits for them, and re-layouts: 1.99 us -> none
    pallas_call x1, Pallas kernels: 75.2 us -> 74.3 us  [on_device(): pl.pallas_call(functools.partial(kernel, scale, nope, rope, width, value,...]
    pallas_call x0 -> x1, Pallas kernels: none -> 0.86 us  [on_device(): pl.pallas_call(functools.partial(write_kernel, rope), out_shape=(jax.Shap...]
where the time goes in v4:
time: 76 us; the launch traced here: 75.8 us
  Pallas kernels  75.2 us (99%)
    pallas_call x1, Pallas kernels, on_device(): pl.pallas_call(functools.partial(kernel, scale, nope, rope, width, value,...  74.3 us

profile of v4, /device:TPU:1, one launch (start us, length us, event | category | flops | bytes accessed | tf_op | source)
XLA Modules:
  0.0 75.8 jit_solution(17923504325007277455)
XLA Ops:
  0.6 74.3 %shard_map.85 = (bf16[128,256]{1,0:T(8,128)(2,1)S(1)}, bf16[128,384]{1,0:T(8,128)(2,1)S(1)}, bf16[2,2,4,3,16,128]{5,4,3,2,1,0:T(8,128)(2,1)S(1)}) custom-call(s32[32]{0:T(128)} %blocks_hbm.1, bf16[576,128]{1,0:T(8,128)(2,1)} %bitcast.2, bf16[128,384]{1,0:T(8,128)(2,1)} %q_hbm.1, bf16[128,256]{1,0:T(8,128)(2,1)} %g_hbm.1, bf16[2,128,512]{2,1,0:T(8,128)(2,1)} %ku_hbm.1, ...), custom_call_target="tpu_custom_call" | custom-call | tf_op jit(solution)/shard_map/pallas_call | solution.py:477
  75.0 0.9 %shard_map.86 = (bf16[128,256]{1,0:T(8,128)(2,1)}, bf16[128,384]{1,0:T(8,128)(2,1)}, f32[576,128]{1,0:T(8,128)}) custom-call(bf16[128,256]{1,0:T(8,128)(2,1)S(1)} %get-tuple-element.9.att, bf16[128,384]{1,0:T(8,128)(2,1)S(1)} %get-tuple-element.10.qg, bf16[2,2,4,3,16,128]{5,4,3,2,1,0:T(8,128)(2,1)S(1)} %get-tuple-element.11.final), custom_call_target="tpu_custom_call" | custom-call | tf_op jit(solution)/shard_map/pallas_call | solution.py:533

commit v5 on v4

--- a/solution.py
+++ b/solution.py
@@ -15,6 +15,7 @@
 SLOTS = (0, 1, 7, 2, 6, 3, 5, 4)
 SLOT_OF = {j: i for i, j in enumerate(SLOTS)}
 HALF = NY // 2
+SPANS = ((0, 2, 3), (3, 4, 5), (5, 6, 8))
 GROUPS = (pl.ds(0, HALF), pl.ds(HALF, HALF))
 TILE_OF = ((0, 1, 5, 6), (2, 3, 7, 8))
 ROTARY_TILE = 4
@@ -83,6 +84,7 @@
         dict(pair=pair, dk=dk, dx=dx)
         for pair in range(2) for dk in range(NC) for dx in range(NX) if pair or dk or dx
     ]
+    finals.sort(key=lambda p: -(p["pair"] + min(p["dx"], NX - p["dx"])))
     peers = (
         [dict(dy=d) for d in range(1, NY)]
         + [dict(dy=d, pair=1) for d in range(1, NY)]
@@ -139,21 +141,22 @@
         )
 
     def spread(zr, group, arrivals):
-        for j in SLOTS[group * HALF : (group + 1) * HALF]:
+        start, _, stop = SPANS[group]
+        for j in SLOTS[start:stop]:
             if j:
                 arrivals[j].wait_recv()
-        part = GROUPS[group]
+        part = pl.ds(start, stop - start)
         return (
             x_copy(zr, 4 * group, 0, 3, part, 1),
             x_copy(zr, 4 * group + 1, 0, 1, part, 3),
         )
 
     def relay(zr, group, moves):
-        start = group * HALF
+        start, middle, stop = SPANS[group]
         moves[0].wait_recv()
-        right = x_copy(zr, 4 * group + 2, 3, 2, pl.ds(start, HALF // 2), 1)
+        right = x_copy(zr, 4 * group + 2, 3, 2, pl.ds(start, middle - start), 1)
         moves[1].wait_recv()
-        left = x_copy(zr, 4 * group + 3, 1, 2, pl.ds(start + HALF // 2, HALF // 2), 3)
+        left = x_copy(zr, 4 * group + 3, 1, 2, pl.ds(middle, stop - middle), 3)
         return right, left
 
     def close(zr, *relays):
@@ -218,29 +221,30 @@
                 )
         starts.append(start + lax.rem(lane, SR))
 
-    near_a = spread(0, 0, near)
+    near_moves = [spread(0, 0, near), spread(0, 1, near)]
     to_mirror.wait_recv()
     far = along_y(1, keys.at[1, 0, 0, 0])
-    near_b = spread(0, 1, near)
+    near_moves.append(spread(0, 2, near))
     across = {(0, 0): cross(0, 0)}
-    near_relay_a = relay(0, 0, near_a)
-    far_a = spread(1, 0, far)
-    near_relay_b = relay(0, 1, near_b)
+    near_relays = relay(0, 0, near_moves[0]) + relay(0, 1, near_moves[1])
+    far_moves = [spread(1, 0, far)]
+    near_relays += relay(0, 2, near_moves[2])
     across[0, 3] = cross(0, 3)
     across[0, 1] = cross(0, 1)
     score(0, 0, across[0, 0])
-    far_b = spread(1, 1, far)
+    far_moves += [spread(1, 1, far), spread(1, 2, far)]
     across[1, 0] = cross(1, 0)
-    across[0, 2] = close(0, *near_relay_a, *near_relay_b)
-    far_relay_a = relay(1, 0, far_a)
+    far_relays = relay(1, 0, far_moves[0])
+    across[0, 2] = close(0, *near_relays)
     score(0, 3, across[0, 3])
+    far_relays += relay(1, 1, far_moves[1])
     score(0, 1, across[0, 1])
-    far_relay_b = relay(1, 1, far_b)
+    far_relays += relay(1, 2, far_moves[2])
     across[1, 3] = cross(1, 3)
     across[1, 1] = cross(1, 1)
     score(0, 2, across[0, 2])
     score(1, 0, across[1, 0])
-    across[1, 2] = close(1, *far_relay_a, *far_relay_b)
+    across[1, 2] = close(1, *far_relays)
     score(1, 3, across[1, 3])
     score(1, 1, across[1, 1])
     score(1, 2, across[1, 2])
@@ -334,7 +338,6 @@
     pair_sum(3)
     direct(0)
     opposite(1)
-    crossings[0].wait_recv()
 
     out = jnp.zeros((both, width), F32)
     step = 2 * chunk
@@ -375,6 +378,7 @@
         second = base[HALF:] + direct_in[0, at].astype(F32) + sum_in[1, at].astype(F32)
         return jnp.concatenate([first, second], axis=0).astype(BF)
 
+    crossings[0].wait_recv()
     for i in range(2, 6):
         hops[0, i].wait_recv()
     for i in range(WIDE):
@@ -517,7 +521,7 @@
             pltpu.VMEM((3, 3, *tile), BF),
             dma((2, NY - 1)), dma((2, NY - 1)),
             dma, dma,
-            dma((2, 8)), dma((2, 8)),
+            dma((2, 12)), dma((2, 12)),
             dma((2, NX)), dma((2, NX)),
             dma((NX,)), dma((NX,)),
             dma((2, 6)), dma((2, 6)),

time: 76 us -> 75.4 us (level)
  no operation moved by 1% of the time
where the time goes in v5:
time: 75.4 us; the launch traced here: 75.3 us
  Pallas kernels  74.6 us (99%)
    pallas_call x1, Pallas kernels, on_device(): pl.pallas_call(functools.partial(kernel, scale, nope, rope, width, value,...  73.8 us

profile of v5, /device:TPU:1, one launch (start us, length us, event | category | flops | bytes accessed | tf_op | source)
XLA Modules:
  0.0 75.3 jit_solution(3456003970957996250)
XLA Ops:
  0.6 73.8 %shard_map.85 = (bf16[128,256]{1,0:T(8,128)(2,1)S(1)}, bf16[128,384]{1,0:T(8,128)(2,1)S(1)}, bf16[2,2,4,3,16,128]{5,4,3,2,1,0:T(8,128)(2,1)S(1)}) custom-call(s32[32]{0:T(128)} %blocks_hbm.1, bf16[576,128]{1,0:T(8,128)(2,1)} %bitcast.2, bf16[128,384]{1,0:T(8,128)(2,1)} %q_hbm.1, bf16[128,256]{1,0:T(8,128)(2,1)} %g_hbm.1, bf16[2,128,512]{2,1,0:T(8,128)(2,1)} %ku_hbm.1, ...), custom_call_target="tpu_custom_call" | custom-call | tf_op jit(solution)/shard_map/pallas_call | solution.py:481
  74.4 0.9 %shard_map.86 = (bf16[128,256]{1,0:T(8,128)(2,1)}, bf16[128,384]{1,0:T(8,128)(2,1)}, f32[576,128]{1,0:T(8,128)}) custom-call(bf16[128,256]{1,0:T(8,128)(2,1)S(1)} %get-tuple-element.9.att, bf16[128,384]{1,0:T(8,128)(2,1)S(1)} %get-tuple-element.10.qg, bf16[2,2,4,3,16,128]{5,4,3,2,1,0:T(8,128)(2,1)S(1)} %get-tuple-element.11.final), custom_call_target="tpu_custom_call" | custom-call | tf_op jit(solution)/shard_map/pallas_call | solution.py:537
